TPU v7x, 256 devices: a whole 4x4x8 slice. The times are simulated.
256 devices in a mesh: sec: 8 (over x, core), row: 32 (over z, y).
Axes of the slice: x: 4, y: 4, z: 8, core: 2. Of those that a mesh axis runs over, the one named last changes fastest.
Arguments:
- factor: float32 [8, 2048, 16384], P(None, 'row', 'sec'), may hold values from -0.046875 to 0.046875
- inverse_blocks: float32 [8, 2048, 2048], P('sec', 'row'), may hold values from -4 to 4, as said below
- right_side: float32 [8, 2048, 384], P('sec', 'row'), may hold values from -6 to 6
Outputs:
- solution: float32 [8, 2048, 384], P('sec', 'row')
Inputs may be any that keep to these rules, and one draw needn't show every extreme that they name: `inverse_blocks`: each block is nonsingular; it stands for the inverse of the factor's diagonal block of that section.
All inputs are finite; a program needn't handle non-finite values.
Results may differ from a plain program's by a relative error of at most 0.0001.
Values sent between devices are 32-bit elements; how exact they have to be, the bound alone decides.
No kernel may reach another device: no remote copies, remote signals or barrier semaphores. Data moves between devices by JAX's collectives and lax.ppermute only.
A program may use at most 64 MiB of HBM per device.

v0:
```python
import jax
import jax.numpy as jnp
from jax import lax
from jax.sharding import PartitionSpec as P

MICRO = 3
WIDTH = 128


highest = lax.Precision.HIGHEST


def sent_to_all(shard, axis):
    size = lax.axis_size(axis)
    return lax.all_to_all(
        jnp.broadcast_to(shard[None], (size, *shard.shape)), axis, 0, 0, tiled=True
    )


def laid_out(blocks, dim):
    shape = list(blocks.shape[1:])
    shape[dim] *= blocks.shape[0]
    return jnp.moveaxis(blocks, 0, dim).reshape(shape)


def collect(shard, axis, dim):
    blocks = sent_to_all(shard, axis)
    return laid_out(blocks, dim)


def passed_along(block, axis, distance):
    devices = range(lax.axis_size(axis))
    route = [(i - distance, i) for i in devices if i - distance in devices]
    return lax.ppermute(block, axis, route)


def shards(factor, inverse_blocks, right_side):
    sections = lax.axis_size("sec")
    segment = lax.axis_index("sec")
    local_rows = factor.shape[1]
    block_cols = factor.shape[2]
    width = WIDTH
    own_inverse = inverse_blocks[0]
    panel_rows = factor.reshape(sections * local_rows, block_cols)
    combined = jnp.dot(
        panel_rows, lax.all_gather(own_inverse, "row", axis=0, tiled=True), precision=highest
    )

    def advance(tick_index, state):
        carried, head, solution = state
        group = tick_index - segment
        valid = jnp.logical_and(group >= 0, group < MICRO)
        clipped = jnp.clip(group, 0, MICRO - 1)
        start_col = clipped * width
        own_rhs = lax.dynamic_slice_in_dim(right_side[0], start_col, width, 1)
        own_sum = lax.dynamic_index_in_dim(carried, segment, 0, keepdims=False)
        residual = own_rhs - own_sum
        full_residual = collect(residual, "row", 0)
        own_result = jnp.dot(own_inverse, full_residual, precision=highest)
        updated = lax.dynamic_update_slice_in_dim(solution, own_result, start_col, 1)
        solution = jnp.where(valid, updated, solution)
        flat_in = carried.reshape(sections * local_rows, width)
        outgoing = flat_in + jnp.dot(combined, full_residual, precision=highest)
        outgoing = outgoing.reshape(sections, local_rows, width)
        carried = passed_along(outgoing, "sec", 1)
        return (carried, head, solution)

    initial = (
        jnp.zeros((sections, local_rows, width), jnp.float32),
        jnp.zeros((local_rows, width), jnp.float32),
        jnp.zeros(right_side.shape[1:], jnp.float32),
    )
    final = lax.fori_loop(0, sections + MICRO - 1, advance, initial)
    return final[2][None]


def solution(mesh):
    return jax.shard_map(
        shards,
        mesh=mesh,
        in_specs=(P(None, "row", "sec"), P("sec", "row", None), P("sec", "row", None)),
        out_specs=P("sec", "row", None),
        check_vma=False,
    )
```

profile of v0, /device:TPU:1, one launch (start us, length us, event | category | flops | bytes accessed | tf_op | source)
XLA Modules:
  0.0 661.3 jit_solution(8280673327536121644)
XLA Ops:
  7.3 145.4 %all-gather.3.cloned.1.call-done = f32[1,2048,2048]{2,1,0:T(8,128)} async-done(((f32[1,64,2048]{2,1,0:T(8,128)}), f32[1,2048,2048]{2,1,0:T(8,128)}) %all-gather.3.cloned.1.call-update) | async-done | bytes 16777232 | tf_op jit(solution)/shard_map/all_gather | solution.py:46
  152.7 32.3 %fusion.3 = f32[512,2048]{1,0:T(8,128)} fusion(f32[512,2048]{1,0:T(8,128)} %bitcast.51, f32[1,2048,2048]{2,1,0:T(8,128)} %all-gather.3.cloned.1.call-done), kind=kOutput, calls=%fused_computation.6 | convolution fusion | flops 25769803776 | bytes 25165824 | tf_op jit(solution)/shard_map/dot_general | solution.py:45
  185.1 468.8 %while.17 = (s32[]{:T(128)}, f32[8,64,128]{2,1,0:T(8,128)S(1)}, f32[64,384]{1,0:T(8,128)S(1)}, s32[]{:T(128)}, f32[1,64,384]{2,1,0:T(8,128)}, /*index=5*/s32[]{:...) while((s32[]{:T(128)}, f32[8,64,128]{2,1,0:T(8,128)S(1)}, ...), condition=%wide.region_1.2_spmd, body=%wide.region_0.1_spmd.sunk | while | flops 1812021248 | bytes 13828417 | solution.py:73
  192.5 25.7 %all-to-all-done = f32[32,64,128]{2,1,0:T(8,128)S(1)} async-done(((f32[32,64,128]{2,1,0:T(8,128)}), f32[32,64,128]{2,1,0:T(8,128)S(1)}, u32[]{:S(2)}, u32[]{:S(2)}) %all-to-all-start) | async-done | bytes 1048608 | tf_op jit(solution)/shard_map/while/body/eval_jaxpr/all_to_all | solution.py:15
  241.7 25.1 %all-to-all-done = f32[32,64,128]{2,1,0:T(8,128)S(1)} async-done(((f32[32,64,128]{2,1,0:T(8,128)}), f32[32,64,128]{2,1,0:T(8,128)S(1)}, u32[]{:S(2)}, u32[]{:S(2)}) %all-to-all-start) | async-done | bytes 1048608 | tf_op jit(solution)/shard_map/while/body/eval_jaxpr/all_to_all | solution.py:15
  273.5 6.8 %collective-permute-start = (f32[8,64,128]{2,1,0:T(8,128)S(1)}, f32[8,64,128]{2,1,0:T(8,128)S(1)}, u32[]{:S(2)}, u32[]{:S(2)}) collective-permute-start(f32[8,64,128]{2,1,0:T(8,128)S(1)} %bitcast.50), channel_id=1, source_target_pairs={{0,32},{32,64},{64,96},{96,128},{128,160},{160,192},{192,224},{1,3... | collective-permute-start | bytes 786440 | tf_op jit(solution)/shard_map/while/body/eval_jaxpr/ppermute | solution.py:34
  290.9 22.5 %all-to-all-done = f32[32,64,128]{2,1,0:T(8,128)S(1)} async-done(((f32[32,64,128]{2,1,0:T(8,128)}), f32[32,64,128]{2,1,0:T(8,128)S(1)}, u32[]{:S(2)}, u32[]{:S(2)}) %all-to-all-start) | async-done | bytes 1048608 | tf_op jit(solution)/shard_map/while/body/eval_jaxpr/all_to_all | solution.py:15
  313.4 6.6 %fusion.20 = f32[512,128]{0,1:T(8,128)S(1)} fusion(f32[512,128]{0,1:T(8,128)S(1)} %copy.10, f32[2048,128]{1,0:T(8,128)S(1)} %bitcast.46, f32[512,2048]{1,0:T(8,128)} %get-tuple-element.289), kind=kOutput, calls=%fused_computation.1.clone.1 | convolution fusion | flops 1610678272 | bytes 5767168 | tf_op jit(solution)/shard_map/while/body/eval_jaxpr/dot_general | solution.py:63
  320.1 9.1 %collective-permute-start = (f32[8,64,128]{2,1,0:T(8,128)S(1)}, f32[8,64,128]{2,1,0:T(8,128)S(1)}, u32[]{:S(2)}, u32[]{:S(2)}) collective-permute-start(f32[8,64,128]{2,1,0:T(8,128)S(1)} %bitcast.50), channel_id=1, source_target_pairs={{0,32},{32,64},{64,96},{96,128},{128,160},{160,192},{192,224},{1,3... | collective-permute-start | bytes 786440 | tf_op jit(solution)/shard_map/while/body/eval_jaxpr/ppermute | solution.py:34
  339.8 20.1 %all-to-all-done = f32[32,64,128]{2,1,0:T(8,128)S(1)} async-done(((f32[32,64,128]{2,1,0:T(8,128)}), f32[32,64,128]{2,1,0:T(8,128)S(1)}, u32[]{:S(2)}, u32[]{:S(2)}) %all-to-all-start) | async-done | bytes 1048608 | tf_op jit(solution)/shard_map/while/body/eval_jaxpr/all_to_all | solution.py:15
  359.9 6.6 %fusion.20 = f32[512,128]{0,1:T(8,128)S(1)} fusion(f32[512,128]{0,1:T(8,128)S(1)} %copy.10, f32[2048,128]{1,0:T(8,128)S(1)} %bitcast.46, f32[512,2048]{1,0:T(8,128)} %get-tuple-element.289), kind=kOutput, calls=%fused_computation.1.clone.1 | convolution fusion | flops 1610678272 | bytes 5767168 | tf_op jit(solution)/shard_map/while/body/eval_jaxpr/dot_general | solution.py:63
  366.7 8.7 %collective-permute-start = (f32[8,64,128]{2,1,0:T(8,128)S(1)}, f32[8,64,128]{2,1,0:T(8,128)S(1)}, u32[]{:S(2)}, u32[]{:S(2)}) collective-permute-start(f32[8,64,128]{2,1,0:T(8,128)S(1)} %bitcast.50), channel_id=1, source_target_pairs={{0,32},{32,64},{64,96},{96,128},{128,160},{160,192},{192,224},{1,3... | collective-permute-start | bytes 786440 | tf_op jit(solution)/shard_map/while/body/eval_jaxpr/ppermute | solution.py:34
  385.9 20.6 %all-to-all-done = f32[32,64,128]{2,1,0:T(8,128)S(1)} async-done(((f32[32,64,128]{2,1,0:T(8,128)}), f32[32,64,128]{2,1,0:T(8,128)S(1)}, u32[]{:S(2)}, u32[]{:S(2)}) %all-to-all-start) | async-done | bytes 1048608 | tf_op jit(solution)/shard_map/while/body/eval_jaxpr/all_to_all | solution.py:15
  406.4 6.6 %fusion.20 = f32[512,128]{0,1:T(8,128)S(1)} fusion(f32[512,128]{0,1:T(8,128)S(1)} %copy.10, f32[2048,128]{1,0:T(8,128)S(1)} %bitcast.46, f32[512,2048]{1,0:T(8,128)} %get-tuple-element.289), kind=kOutput, calls=%fused_computation.1.clone.1 | convolution fusion | flops 1610678272 | bytes 5767168 | tf_op jit(solution)/shard_map/while/body/eval_jaxpr/dot_general | solution.py:63
  413.2 8.0 %collective-permute-start = (f32[8,64,128]{2,1,0:T(8,128)S(1)}, f32[8,64,128]{2,1,0:T(8,128)S(1)}, u32[]{:S(2)}, u32[]{:S(2)}) collective-permute-start(f32[8,64,128]{2,1,0:T(8,128)S(1)} %bitcast.50), channel_id=1, source_target_pairs={{0,32},{32,64},{64,96},{96,128},{128,160},{160,192},{192,224},{1,3... | collective-permute-start | bytes 786440 | tf_op jit(solution)/shard_map/while/body/eval_jaxpr/ppermute | solution.py:34
  431.7 21.3 %all-to-all-done = f32[32,64,128]{2,1,0:T(8,128)S(1)} async-done(((f32[32,64,128]{2,1,0:T(8,128)}), f32[32,64,128]{2,1,0:T(8,128)S(1)}, u32[]{:S(2)}, u32[]{:S(2)}) %all-to-all-start) | async-done | bytes 1048608 | tf_op jit(solution)/shard_map/while/body/eval_jaxpr/all_to_all | solution.py:15
  459.8 7.3 %collective-permute-start = (f32[8,64,128]{2,1,0:T(8,128)S(1)}, f32[8,64,128]{2,1,0:T(8,128)S(1)}, u32[]{:S(2)}, u32[]{:S(2)}) collective-permute-start(f32[8,64,128]{2,1,0:T(8,128)S(1)} %bitcast.50), channel_id=1, source_target_pairs={{0,32},{32,64},{64,96},{96,128},{128,160},{160,192},{192,224},{1,3... | collective-permute-start | bytes 786440 | tf_op jit(solution)/shard_map/while/body/eval_jaxpr/ppermute | solution.py:34
  477.6 21.8 %all-to-all-done = f32[32,64,128]{2,1,0:T(8,128)S(1)} async-done(((f32[32,64,128]{2,1,0:T(8,128)}), f32[32,64,128]{2,1,0:T(8,128)S(1)}, u32[]{:S(2)}, u32[]{:S(2)}) %all-to-all-start) | async-done | bytes 1048608 | tf_op jit(solution)/shard_map/while/body/eval_jaxpr/all_to_all | solution.py:15
  506.2 6.7 %collective-permute-start = (f32[8,64,128]{2,1,0:T(8,128)S(1)}, f32[8,64,128]{2,1,0:T(8,128)S(1)}, u32[]{:S(2)}, u32[]{:S(2)}) collective-permute-start(f32[8,64,128]{2,1,0:T(8,128)S(1)} %bitcast.50), channel_id=1, source_target_pairs={{0,32},{32,64},{64,96},{96,128},{128,160},{160,192},{192,224},{1,3... | collective-permute-start | bytes 786440 | tf_op jit(solution)/shard_map/while/body/eval_jaxpr/ppermute | solution.py:34
  523.4 22.6 %all-to-all-done = f32[32,64,128]{2,1,0:T(8,128)S(1)} async-done(((f32[32,64,128]{2,1,0:T(8,128)}), f32[32,64,128]{2,1,0:T(8,128)S(1)}, u32[]{:S(2)}, u32[]{:S(2)}) %all-to-all-start) | async-done | bytes 1048608 | tf_op jit(solution)/shard_map/while/body/eval_jaxpr/all_to_all | solution.py:15
  546.1 6.6 %fusion.20 = f32[512,128]{0,1:T(8,128)S(1)} fusion(f32[512,128]{0,1:T(8,128)S(1)} %copy.10, f32[2048,128]{1,0:T(8,128)S(1)} %bitcast.46, f32[512,2048]{1,0:T(8,128)} %get-tuple-element.289), kind=kOutput, calls=%fused_computation.1.clone.1 | convolution fusion | flops 1610678272 | bytes 5767168 | tf_op jit(solution)/shard_map/while/body/eval_jaxpr/dot_general | solution.py:63
  569.3 23.3 %all-to-all-done = f32[32,64,128]{2,1,0:T(8,128)S(1)} async-done(((f32[32,64,128]{2,1,0:T(8,128)}), f32[32,64,128]{2,1,0:T(8,128)S(1)}, u32[]{:S(2)}, u32[]{:S(2)}) %all-to-all-start) | async-done | bytes 1048608 | tf_op jit(solution)/shard_map/while/body/eval_jaxpr/all_to_all | solution.py:15
  592.6 6.6 %fusion.20 = f32[512,128]{0,1:T(8,128)S(1)} fusion(f32[512,128]{0,1:T(8,128)S(1)} %copy.10, f32[2048,128]{1,0:T(8,128)S(1)} %bitcast.46, f32[512,2048]{1,0:T(8,128)} %get-tuple-element.289), kind=kOutput, calls=%fused_computation.1.clone.1 | convolution fusion | flops 1610678272 | bytes 5767168 | tf_op jit(solution)/shard_map/while/body/eval_jaxpr/dot_general | solution.py:63
  615.2 24.1 %all-to-all-done = f32[32,64,128]{2,1,0:T(8,128)S(1)} async-done(((f32[32,64,128]{2,1,0:T(8,128)}), f32[32,64,128]{2,1,0:T(8,128)S(1)}, u32[]{:S(2)}, u32[]{:S(2)}) %all-to-all-start) | async-done | bytes 1048608 | tf_op jit(solution)/shard_map/while/body/eval_jaxpr/all_to_all | solution.py:15
  (87 shorter events, 162.7 us)
Async XLA Ops:
  6.5 146.2 %all-gather.3.cloned.1.call-start = ((), (), s32[]{:S(2)}) async-start(), calls=%async_computation.1 | async-start | bytes 17301504 | tf_op jit(solution)/shard_map/all_gather | solution.py:46
  152.7 32.3 %copy-start = (f32[1,64,2048]{2,1,0:T(8,128)S(1)}, f32[1,64,2048]{2,1,0:T(8,128)}, u32[]{:S(2)}) copy-start(f32[1,64,2048]{2,1,0:T(8,128)} %param.6) | copy-start | bytes 1572868
  186.9 31.2 %all-to-all-start = ((f32[32,64,128]{2,1,0:T(8,128)}), f32[32,64,128]{2,1,0:T(8,128)S(1)}, u32[]{:S(2)}, u32[]{:S(2)}) async-start(f32[32,64,128]{2,1,0:T(8,128)} %broadcast_in_dim.37), calls=%async_computation | async-start | bytes 2097152 | tf_op jit(solution)/shard_map/while/body/eval_jaxpr/all_to_all | solution.py:15
  224.9 9.5 %collective-permute-start = (f32[8,64,128]{2,1,0:T(8,128)S(1)}, f32[8,64,128]{2,1,0:T(8,128)S(1)}, u32[]{:S(2)}, u32[]{:S(2)}) collective-permute-start(f32[8,64,128]{2,1,0:T(8,128)S(1)} %bitcast.50), channel_id=1, source_target_pairs={{0,32},{32,64},{64,96},{96,128},{128,160},{160,192},{192,224},{1,3... | collective-permute-start | bytes 786440 | tf_op jit(solution)/shard_map/while/body/eval_jaxpr/ppermute | solution.py:34
  236.2 30.5 %all-to-all-start = ((f32[32,64,128]{2,1,0:T(8,128)}), f32[32,64,128]{2,1,0:T(8,128)S(1)}, u32[]{:S(2)}, u32[]{:S(2)}) async-start(f32[32,64,128]{2,1,0:T(8,128)} %broadcast_in_dim.37), calls=%async_computation | async-start | bytes 2097152 | tf_op jit(solution)/shard_map/while/body/eval_jaxpr/all_to_all | solution.py:15
  273.5 10.1 %collective-permute-start = (f32[8,64,128]{2,1,0:T(8,128)S(1)}, f32[8,64,128]{2,1,0:T(8,128)S(1)}, u32[]{:S(2)}, u32[]{:S(2)}) collective-permute-start(f32[8,64,128]{2,1,0:T(8,128)S(1)} %bitcast.50), channel_id=1, source_target_pairs={{0,32},{32,64},{64,96},{96,128},{128,160},{160,192},{192,224},{1,3... | collective-permute-start | bytes 786440 | tf_op jit(solution)/shard_map/while/body/eval_jaxpr/ppermute | solution.py:34
  285.4 27.9 %all-to-all-start = ((f32[32,64,128]{2,1,0:T(8,128)}), f32[32,64,128]{2,1,0:T(8,128)S(1)}, u32[]{:S(2)}, u32[]{:S(2)}) async-start(f32[32,64,128]{2,1,0:T(8,128)} %broadcast_in_dim.37), calls=%async_computation | async-start | bytes 2097152 | tf_op jit(solution)/shard_map/while/body/eval_jaxpr/all_to_all | solution.py:15
  320.1 12.4 %collective-permute-start = (f32[8,64,128]{2,1,0:T(8,128)S(1)}, f32[8,64,128]{2,1,0:T(8,128)S(1)}, u32[]{:S(2)}, u32[]{:S(2)}) collective-permute-start(f32[8,64,128]{2,1,0:T(8,128)S(1)} %bitcast.50), channel_id=1, source_target_pairs={{0,32},{32,64},{64,96},{96,128},{128,160},{160,192},{192,224},{1,3... | collective-permute-start | bytes 786440 | tf_op jit(solution)/shard_map/while/body/eval_jaxpr/ppermute | solution.py:34
  334.3 25.6 %all-to-all-start = ((f32[32,64,128]{2,1,0:T(8,128)}), f32[32,64,128]{2,1,0:T(8,128)S(1)}, u32[]{:S(2)}, u32[]{:S(2)}) async-start(f32[32,64,128]{2,1,0:T(8,128)} %broadcast_in_dim.37), calls=%async_computation | async-start | bytes 2097152 | tf_op jit(solution)/shard_map/while/body/eval_jaxpr/all_to_all | solution.py:15
  366.7 12.0 %collective-permute-start = (f32[8,64,128]{2,1,0:T(8,128)S(1)}, f32[8,64,128]{2,1,0:T(8,128)S(1)}, u32[]{:S(2)}, u32[]{:S(2)}) collective-permute-start(f32[8,64,128]{2,1,0:T(8,128)S(1)} %bitcast.50), channel_id=1, source_target_pairs={{0,32},{32,64},{64,96},{96,128},{128,160},{160,192},{192,224},{1,3... | collective-permute-start | bytes 786440 | tf_op jit(solution)/shard_map/while/body/eval_jaxpr/ppermute | solution.py:34
  380.5 25.9 %all-to-all-start = ((f32[32,64,128]{2,1,0:T(8,128)}), f32[32,64,128]{2,1,0:T(8,128)S(1)}, u32[]{:S(2)}, u32[]{:S(2)}) async-start(f32[32,64,128]{2,1,0:T(8,128)} %broadcast_in_dim.37), calls=%async_computation | async-start | bytes 2097152 | tf_op jit(solution)/shard_map/while/body/eval_jaxpr/all_to_all | solution.py:15
  413.2 11.3 %collective-permute-start = (f32[8,64,128]{2,1,0:T(8,128)S(1)}, f32[8,64,128]{2,1,0:T(8,128)S(1)}, u32[]{:S(2)}, u32[]{:S(2)}) collective-permute-start(f32[8,64,128]{2,1,0:T(8,128)S(1)} %bitcast.50), channel_id=1, source_target_pairs={{0,32},{32,64},{64,96},{96,128},{128,160},{160,192},{192,224},{1,3... | collective-permute-start | bytes 786440 | tf_op jit(solution)/shard_map/while/body/eval_jaxpr/ppermute | solution.py:34
  426.4 26.6 %all-to-all-start = ((f32[32,64,128]{2,1,0:T(8,128)}), f32[32,64,128]{2,1,0:T(8,128)S(1)}, u32[]{:S(2)}, u32[]{:S(2)}) async-start(f32[32,64,128]{2,1,0:T(8,128)} %broadcast_in_dim.37), calls=%async_computation | async-start | bytes 2097152 | tf_op jit(solution)/shard_map/while/body/eval_jaxpr/all_to_all | solution.py:15
  459.8 10.6 %collective-permute-start = (f32[8,64,128]{2,1,0:T(8,128)S(1)}, f32[8,64,128]{2,1,0:T(8,128)S(1)}, u32[]{:S(2)}, u32[]{:S(2)}) collective-permute-start(f32[8,64,128]{2,1,0:T(8,128)S(1)} %bitcast.50), channel_id=1, source_target_pairs={{0,32},{32,64},{64,96},{96,128},{128,160},{160,192},{192,224},{1,3... | collective-permute-start | bytes 786440 | tf_op jit(solution)/shard_map/while/body/eval_jaxpr/ppermute | solution.py:34
  472.2 27.2 %all-to-all-start = ((f32[32,64,128]{2,1,0:T(8,128)}), f32[32,64,128]{2,1,0:T(8,128)S(1)}, u32[]{:S(2)}, u32[]{:S(2)}) async-start(f32[32,64,128]{2,1,0:T(8,128)} %broadcast_in_dim.37), calls=%async_computation | async-start | bytes 2097152 | tf_op jit(solution)/shard_map/while/body/eval_jaxpr/all_to_all | solution.py:15
  506.2 10.0 %collective-permute-start = (f32[8,64,128]{2,1,0:T(8,128)S(1)}, f32[8,64,128]{2,1,0:T(8,128)S(1)}, u32[]{:S(2)}, u32[]{:S(2)}) collective-permute-start(f32[8,64,128]{2,1,0:T(8,128)S(1)} %bitcast.50), channel_id=1, source_target_pairs={{0,32},{32,64},{64,96},{96,128},{128,160},{160,192},{192,224},{1,3... | collective-permute-start | bytes 786440 | tf_op jit(solution)/shard_map/while/body/eval_jaxpr/ppermute | solution.py:34
  518.1 28.0 %all-to-all-start = ((f32[32,64,128]{2,1,0:T(8,128)}), f32[32,64,128]{2,1,0:T(8,128)S(1)}, u32[]{:S(2)}, u32[]{:S(2)}) async-start(f32[32,64,128]{2,1,0:T(8,128)} %broadcast_in_dim.37), calls=%async_computation | async-start | bytes 2097152 | tf_op jit(solution)/shard_map/while/body/eval_jaxpr/all_to_all | solution.py:15
  552.8 9.3 %collective-permute-start = (f32[8,64,128]{2,1,0:T(8,128)S(1)}, f32[8,64,128]{2,1,0:T(8,128)S(1)}, u32[]{:S(2)}, u32[]{:S(2)}) collective-permute-start(f32[8,64,128]{2,1,0:T(8,128)S(1)} %bitcast.50), channel_id=1, source_target_pairs={{0,32},{32,64},{64,96},{96,128},{128,160},{160,192},{192,224},{1,3... | collective-permute-start | bytes 786440 | tf_op jit(solution)/shard_map/while/body/eval_jaxpr/ppermute | solution.py:34
  563.9 28.7 %all-to-all-start = ((f32[32,64,128]{2,1,0:T(8,128)}), f32[32,64,128]{2,1,0:T(8,128)S(1)}, u32[]{:S(2)}, u32[]{:S(2)}) async-start(f32[32,64,128]{2,1,0:T(8,128)} %broadcast_in_dim.37), calls=%async_computation | async-start | bytes 2097152 | tf_op jit(solution)/shard_map/while/body/eval_jaxpr/all_to_all | solution.py:15
  599.4 8.6 %collective-permute-start = (f32[8,64,128]{2,1,0:T(8,128)S(1)}, f32[8,64,128]{2,1,0:T(8,128)S(1)}, u32[]{:S(2)}, u32[]{:S(2)}) collective-permute-start(f32[8,64,128]{2,1,0:T(8,128)S(1)} %bitcast.50), channel_id=1, source_target_pairs={{0,32},{32,64},{64,96},{96,128},{128,160},{160,192},{192,224},{1,3... | collective-permute-start | bytes 786440 | tf_op jit(solution)/shard_map/while/body/eval_jaxpr/ppermute | solution.py:34
  609.8 29.5 %all-to-all-start = ((f32[32,64,128]{2,1,0:T(8,128)}), f32[32,64,128]{2,1,0:T(8,128)S(1)}, u32[]{:S(2)}, u32[]{:S(2)}) async-start(f32[32,64,128]{2,1,0:T(8,128)} %broadcast_in_dim.37), calls=%async_computation | async-start | bytes 2097152 | tf_op jit(solution)/shard_map/while/body/eval_jaxpr/all_to_all | solution.py:15
  646.1 7.7 %collective-permute-start = (f32[8,64,128]{2,1,0:T(8,128)S(1)}, f32[8,64,128]{2,1,0:T(8,128)S(1)}, u32[]{:S(2)}, u32[]{:S(2)}) collective-permute-start(f32[8,64,128]{2,1,0:T(8,128)S(1)} %bitcast.50), channel_id=1, source_target_pairs={{0,32},{32,64},{64,96},{96,128},{128,160},{160,192},{192,224},{1,3... | collective-permute-start | bytes 786440 | tf_op jit(solution)/shard_map/while/body/eval_jaxpr/ppermute | solution.py:34
  653.8 0.6 copy-start.1
Sparse Core Ops, SparseCore 0:
  9.9 142.7 all-gather.2
where the time goes:
time: 664 us; the launch traced here: 661 us
  waiting for transfers between devices  398 us (60%)
  starting transfers between devices  121 us (18%)
  matrix products  106 us (16%)
  local copies, waits for them, and re-layouts  14 us (2%)
  between operations  13.4 us (2%)
  other arithmetic  7.63 us (1%)
    all_to_all x10, waiting for transfers between devices, sent_to_all(): lax.all_to_all(jnp.broadcast_to(shard[None], (size, *shard.shape)), axis,...  227 us
    all_gather x1, waiting for transfers between devices, shards(): lax.all_gather(own_inverse, 'row', axis=0, tiled=True)  145 us
    ppermute x10, starting transfers between devices, passed_along(): return lax.ppermute(block, axis, route)  68.4 us
    dot_general x10, matrix products, advance(): outgoing = flat_in + jnp.dot(combined, full_residual, precision=highest)  66.3 us
    all_to_all x10, starting transfers between devices, sent_to_all(): lax.all_to_all(jnp.broadcast_to(shard[None], (size, *shard.shape)), axis,...  52.5 us
    dot_general x1, matrix products, shards(): jnp.dot(panel_rows, lax.all_gather(own_inverse, 'row', axis=0, tiled=True...  32.3 us
    ppermute x10, waiting for transfers between devices, passed_along(): return lax.ppermute(block, axis, route)  25 us
  transfers between devices with their start and end apart: 21, of which 21 were waited for; matrix products, arithmetic and copies ran while one was open for 1% of the time, Pallas kernels for 0%

commit v1 on v0

v1 whole, which is shorter than its diff:
```python
import functools

import jax
import jax.numpy as jnp
from jax import lax
from jax.experimental import pallas as pl
from jax.experimental.pallas import tpu as pltpu
from jax.sharding import PartitionSpec as P

LANES = 128
VMEM = pl.BlockSpec(memory_space=pltpu.VMEM)
ANY = pl.BlockSpec(memory_space=pl.ANY)


def low_lanes(shape):
    return lax.broadcasted_iota(jnp.int32, shape, 1) < LANES // 2


def pack_kernel(rhs_ref, out_ref):
    groups, half, _ = out_ref.shape
    rows = rhs_ref[...]
    turned = jnp.concatenate([rows, rows], axis=0).T
    low = low_lanes((half, LANES))
    for group in range(groups):
        start = 2 * group * half
        top = turned[start : start + half]
        bottom = turned[start + half : start + 2 * half]
        out_ref[group] = jnp.where(low, top, bottom)


def unpack_kernel(packed_ref, out_ref):
    groups = packed_ref.shape[0]
    pieces = []
    for group in range(groups):
        tile = packed_ref[group]
        pieces += [tile, pltpu.roll(tile, LANES // 2, 1)]
    turned = jnp.concatenate(pieces, axis=0).T
    out_ref[...] = turned[: LANES // 2]


def split(values):
    high = values.astype(jnp.bfloat16)
    low = (values - high.astype(jnp.float32)).astype(jnp.bfloat16)
    return high, low


def spread(gathered_ref, whole_ref, parts_ref):
    devices, half, _ = gathered_ref.shape
    low = low_lanes((half, LANES))
    for pair in range(devices // 2):
        first = gathered_ref[2 * pair]
        second = gathered_ref[2 * pair + 1]
        lanes = slice(pair * LANES, (pair + 1) * LANES)
        whole_ref[:half, lanes] = jnp.where(low, first, pltpu.roll(second, LANES // 2, 1))
        whole_ref[half:, lanes] = jnp.where(low, pltpu.roll(first, LANES // 2, 1), second)
    high, rest = split(whole_ref[...])
    parts_ref[: 2 * half] = high
    parts_ref[2 * half :] = rest


def times(parts, matrix):
    cols = parts.shape[0] // 2
    high, low = split(matrix)
    dims = (((1,), (1,)), ((), ()))
    both = lax.dot_general(parts, high, dims, preferred_element_type=jnp.float32)
    rest = lax.dot_general(parts[:cols], low, dims, preferred_element_type=jnp.float32)
    return both[:cols] + (both[cols:] + rest)


def packed(turned):
    half = turned.shape[0] // 2
    return jnp.concatenate([turned[:half], turned[half:]], axis=1)


def apply_kernel(index, gathered_ref, matrix_ref, out_ref, block, whole, parts, sem):
    copy = pltpu.make_async_copy(matrix_ref.at[index], block, sem)
    copy.start()
    spread(gathered_ref, whole, parts)
    copy.wait()
    out_ref[...] = packed(times(parts[...], block[...]))


def residual_kernel(index, gathered_ref, base_ref, matrix_ref, out_ref, parts, block, whole, sem):
    copy = pltpu.make_async_copy(matrix_ref.at[index], block, sem)
    copy.start()
    spread(gathered_ref, whole, parts)
    copy.wait()
    out_ref[...] = base_ref[...] - packed(times(parts[...], block[...]))


def earlier_kernel(count, line, *refs):
    base_ref, matrix_ref = refs[:2]
    parts_refs = refs[2 : 2 + count]
    out_ref, blocks, sems = refs[2 + count :]
    copies = []
    for k in range(count):
        copy = pltpu.make_async_copy(matrix_ref.at[(k, line)], blocks.at[k], sems.at[k])
        copy.start()
        copies.append(copy)
    total = None
    for k in range(count):
        copies[k].wait()
        term = times(parts_refs[k][...], blocks[k])
        total = term if total is None else total + term
    out_ref[...] = base_ref[...] - packed(total)


def shards(factor, inverse_blocks, right_side):
    sections = lax.axis_size("sec")
    lines = lax.axis_size("row")
    local_rows, block = factor.shape[1:]
    cols = right_side.shape[2] // sections
    half = cols // 2
    tile = jax.ShapeDtypeStruct((half, LANES), jnp.float32)
    split_shape = (2 * cols, block)
    block_scratch = pltpu.VMEM((local_rows, block), jnp.float32)
    whole_scratch = pltpu.VMEM((cols, block), jnp.float32)
    parts_scratch = pltpu.VMEM(split_shape, jnp.bfloat16)

    inverses = lax.all_gather(inverse_blocks[0], "sec", axis=0)
    rows_of = {}
    for first, last in ((1, 2), (2, 4), (4, 6), (6, 8)):
        panel = lax.all_gather(factor[first:last], "sec", axis=0)
        for j in range(first, min(last, sections)):
            rows_of[j] = (panel, j - first)

    def exchange(shard):
        copies = jnp.broadcast_to(shard[None], (lines, *shard.shape))
        return lax.all_to_all(copies, "row", 0, 0, tiled=True)

    def apply(i, gathered):
        return pl.pallas_call(
            functools.partial(apply_kernel, (i,)),
            out_shape=tile,
            in_specs=[VMEM, ANY],
            out_specs=VMEM,
            scratch_shapes=[block_scratch, whole_scratch, parts_scratch, pltpu.SemaphoreType.DMA],
            name=f"apply_{i}",
        )(gathered, inverses)

    def residual(j, gathered, base):
        panel, line = rows_of[j]
        return pl.pallas_call(
            functools.partial(residual_kernel, (j - 1, line)),
            out_shape=(tile, jax.ShapeDtypeStruct(split_shape, jnp.bfloat16)),
            in_specs=[VMEM, VMEM, ANY],
            out_specs=(VMEM, VMEM),
            scratch_shapes=[block_scratch, whole_scratch, pltpu.SemaphoreType.DMA],
            name=f"residual_{j}",
        )(gathered, base, panel)

    def earlier(j, base, known):
        panel, line = rows_of[j]
        count = len(known)
        return pl.pallas_call(
            functools.partial(earlier_kernel, count, line),
            out_shape=tile,
            in_specs=[VMEM, ANY] + [VMEM] * count,
            out_specs=VMEM,
            scratch_shapes=[
                pltpu.VMEM((count, local_rows, block), jnp.float32),
                pltpu.SemaphoreType.DMA((count,)),
            ],
            name=f"earlier_{j}",
        )(base, panel, *known)

    chunks = pl.pallas_call(
        pack_kernel,
        out_shape=jax.ShapeDtypeStruct((sections, half, LANES), jnp.float32),
        in_specs=[VMEM],
        out_specs=VMEM,
        name="pack",
    )(right_side[0])
    given = lax.all_to_all(chunks, "sec", 0, 0, tiled=True)

    pieces = []
    known = []
    rest = given[0]
    for i in range(sections):
        gathered = exchange(rest)
        piece = apply(i, gathered)
        pieces.append(piece)
        if i + 1 < sections:
            base = given[i + 1]
            gathered = exchange(piece)
            if known:
                base = earlier(i + 1, base, known)
            rest, parts = residual(i + 1, gathered, base)
            known.append(parts)

    found = lax.all_to_all(jnp.stack(pieces), "sec", 0, 0, tiled=True)
    out = pl.pallas_call(
        unpack_kernel,
        out_shape=jax.ShapeDtypeStruct(right_side.shape[1:], jnp.float32),
        in_specs=[VMEM],
        out_specs=VMEM,
        name="unpack",
    )(found)
    return out[None]


def solution(mesh):
    return jax.shard_map(
        shards,
        mesh=mesh,
        in_specs=(P(None, "row", "sec"), P("sec", "row", None), P("sec", "row", None)),
        out_specs=P("sec", "row", None),
        check_vma=False,
    )
```

time: 664 us -> 420 us (0.63)
  waiting for transfers between devices: 398 us -> 89.3 us
  blocking collectives: 0 us -> 171 us
  matrix products: 106 us -> 0 us
  starting transfers between devices: 121 us -> 41.2 us
  Pallas kernels: 0 us -> 72 us
  local copies, waits for them, and re-layouts: 14 us -> 29.5 us
  other arithmetic: 7.63 us -> 0 us
    all_to_all x10 -> x8, waiting for transfers between devices: 227 us -> 48.4 us  [exchange(): return lax.all_to_all(copies, 'row', 0, 0, tiled=True)]
    all_to_all x0 -> x9, blocking collectives: none -> 171 us  [the longest x7 143 us: exchange(): return lax.all_to_all(copies, 'row', 0, 0, tiled=True)]
    dot_general x21 -> x0, matrix products: 106 us -> none  [the longest x10 66.3 us: advance(): outgoing = flat_in + jnp.dot(combined, full_residual, precision=highest)]
    all_gather x1 -> x5, waiting for transfers between devices: 145 us -> 39.1 us  [the longest x4 39.1 us: shards(): panel = lax.all_gather(factor[first:last], 'sec', axis=0)]
    pallas_call x0 -> x22, Pallas kernels: none -> 72 us  [the longest x6 26.1 us: earlier(): pl.pallas_call(functools.partial(earlier_kernel, count, line), out_shape=...]
    ppermute x10 -> x0, starting transfers between devices: 68.4 us -> none  [passed_along(): return lax.ppermute(block, axis, route)]
    ppermute x10 -> x0, waiting for transfers between devices: 25 us -> none  [passed_along(): return lax.ppermute(block, axis, route)]
    all_to_all x10 -> x8, starting transfers between devices: 52.5 us -> 41 us  [exchange(): return lax.all_to_all(copies, 'row', 0, 0, tiled=True)]
  transfers between devices with their start and end apart: 21 -> 13, of which waited for: 21 -> 8; matrix products, arithmetic and copies ran while one was open for 1% -> 5% of each run, Pallas kernels for 0% -> 15%
where the time goes in v1:
time: 420 us; the launch traced here: 417 us
  blocking collectives  171 us (41%)
  waiting for transfers between devices  89.3 us (21%)
  Pallas kernels  72 us (17%)
  starting transfers between devices  41.2 us (10%)
  local copies, waits for them, and re-layouts  29.5 us (7%)
  between operations  13.6 us (3%)
    all_to_all x7, blocking collectives, exchange(): return lax.all_to_all(copies, 'row', 0, 0, tiled=True)  143 us
    all_to_all x8, waiting for transfers between devices, exchange(): return lax.all_to_all(copies, 'row', 0, 0, tiled=True)  48.4 us
    all_to_all x8, starting transfers between devices, exchange(): return lax.all_to_all(copies, 'row', 0, 0, tiled=True)  41 us
    all_gather x4, waiting for transfers between devices, shards(): panel = lax.all_gather(factor[first:last], 'sec', axis=0)  39.1 us
    pallas_call x6, Pallas kernels, earlier(): pl.pallas_call(functools.partial(earlier_kernel, count, line), out_shape=...  26.1 us
    pallas_call x7, Pallas kernels, apply(): pl.pallas_call(functools.partial(apply_kernel, (i,)), out_shape=tile, in_...  21.2 us
    pallas_call x7, Pallas kernels, residual(): pl.pallas_call(functools.partial(residual_kernel, (j - 1, line)), out_sha...  21.2 us
    broadcast_in_dim x15, local copies, waits for them, and re-layouts, exchange(): copies = jnp.broadcast_to(shard[None], (lines, *shard.shape))  16.4 us
  transfers between devices with their start and end apart: 13, of which 8 were waited for; matrix products, arithmetic and copies ran while one was open for 5% of the time, Pallas kernels for 15%

profile of v1, /device:TPU:1, one launch (start us, length us, event | category | flops | bytes accessed | tf_op | source)
XLA Modules:
  0.0 416.5 jit_solution(7254369302532447044)
XLA Ops:
  15.8 11.4 %all_to_all.85 = f32[8,24,128]{2,1,0:T(8,128)S(1)} all-to-all(f32[8,24,128]{2,1,0:T(8,128)} %pack.1), channel_id=1, replica_groups=mesh['sec'=8,'row'=32] {'sec'}, dimensions={0} | all-to-all | bytes 196608 | tf_op jit(solution)/shard_map/all_to_all | solution.py:174
  27.9 24.4 %all_to_all.86.gathered_ref = f32[32,24,128]{2,1,0:T(8,128)} all-to-all(f32[32,24,128]{2,1,0:T(8,128)S(1)} %broadcast_in_dim.35), channel_id=1, replica_groups=mesh['sec'=8,'row'=32] {'row'}, dimensions={0} | all-to-all | bytes 786432 | tf_op jit(solution)/shard_map/all_to_all | solution.py:129
  56.8 5.3 %all-to-all-start.2 = ((f32[32,24,128]{2,1,0:T(8,128)}), f32[32,24,128]{2,1,0:T(8,128)S(1)}, u32[]{:S(2)}, u32[]{:S(2)}) async-start(f32[32,24,128]{2,1,0:T(8,128)} %broadcast_in_dim.36), calls=%async_computation.2 | async-start | bytes 786432 | tf_op jit(solution)/shard_map/all_to_all | solution.py:129
  62.1 22.4 %all-gather.12.cloned.1.call-done = f32[8,64,2048]{2,1,0:T(8,128)} async-done(((f32[1,64,2048]{2,1,0:T(8,128)}), f32[8,64,2048]{2,1,0:T(8,128)}) %all-gather.12.cloned.1.call-update) | async-done | bytes 4194320 | tf_op jit(solution)/shard_map/all_gather | solution.py:123
  89.0 23.6 %all_to_all.87.gathered_ref = f32[32,24,128]{2,1,0:T(8,128)} all-to-all(f32[32,24,128]{2,1,0:T(8,128)S(1)} %broadcast_in_dim.37), channel_id=1, replica_groups=mesh['sec'=8,'row'=32] {'row'}, dimensions={0} | all-to-all | bytes 786432 | tf_op jit(solution)/shard_map/all_to_all | solution.py:129
  121.9 16.7 %all-gather.14.cloned.1.call-done = f32[16,64,2048]{2,1,0:T(8,128)} async-done(((f32[2,64,2048]{2,1,0:T(8,128)}), f32[16,64,2048]{2,1,0:T(8,128)}) %all-gather.14.cloned.1.call-update) | async-done | bytes 8388624 | tf_op jit(solution)/shard_map/all_gather | solution.py:123
  146.1 23.6 %all_to_all.88.gathered_ref = f32[32,24,128]{2,1,0:T(8,128)} all-to-all(f32[32,24,128]{2,1,0:T(8,128)S(1)} %broadcast_in_dim.39), channel_id=1, replica_groups=mesh['sec'=8,'row'=32] {'row'}, dimensions={0} | all-to-all | bytes 786432 | tf_op jit(solution)/shard_map/all_to_all | solution.py:129
  182.6 9.2 %all-to-all-done.6.gathered_ref = f32[32,24,128]{2,1,0:T(8,128)S(1)} async-done(((f32[32,24,128]{2,1,0:T(8,128)}), f32[32,24,128]{2,1,0:T(8,128)S(1)}, u32[]{:S(2)}, u32[]{:S(2)}) %all-to-all-start.6) | async-done | bytes 393248 | tf_op jit(solution)/shard_map/all_to_all | solution.py:129
  196.4 18.3 %all_to_all.89.gathered_ref = f32[32,24,128]{2,1,0:T(8,128)} all-to-all(f32[32,24,128]{2,1,0:T(8,128)S(1)} %broadcast_in_dim.41), channel_id=1, replica_groups=mesh['sec'=8,'row'=32] {'row'}, dimensions={0} | all-to-all | bytes 786432 | tf_op jit(solution)/shard_map/all_to_all | solution.py:129
  219.3 5.8 %all-to-all-start.8 = ((f32[32,24,128]{2,1,0:T(8,128)}), f32[32,24,128]{2,1,0:T(8,128)S(1)}, u32[]{:S(2)}, u32[]{:S(2)}) async-start(f32[32,24,128]{2,1,0:T(8,128)} %broadcast_in_dim.42), calls=%async_computation.8 | async-start | bytes 786432 | tf_op jit(solution)/shard_map/all_to_all | solution.py:129
  229.3 8.4 %all-to-all-done.8.gathered_ref = f32[32,24,128]{2,1,0:T(8,128)S(1)} async-done(((f32[32,24,128]{2,1,0:T(8,128)}), f32[32,24,128]{2,1,0:T(8,128)S(1)}, u32[]{:S(2)}, u32[]{:S(2)}) %all-to-all-start.8) | async-done | bytes 393248 | tf_op jit(solution)/shard_map/all_to_all | solution.py:129
  242.2 18.3 %all_to_all.90.gathered_ref = f32[32,24,128]{2,1,0:T(8,128)} all-to-all(f32[32,24,128]{2,1,0:T(8,128)S(1)} %broadcast_in_dim.43), channel_id=1, replica_groups=mesh['sec'=8,'row'=32] {'row'}, dimensions={0} | all-to-all | bytes 786432 | tf_op jit(solution)/shard_map/all_to_all | solution.py:129
  265.1 5.7 %all-to-all-start.10 = ((f32[32,24,128]{2,1,0:T(8,128)}), f32[32,24,128]{2,1,0:T(8,128)S(1)}, u32[]{:S(2)}, u32[]{:S(2)}) async-start(f32[32,24,128]{2,1,0:T(8,128)} %broadcast_in_dim.44), calls=%async_computation.10 | async-start | bytes 786432 | tf_op jit(solution)/shard_map/all_to_all | solution.py:129
  275.4 7.3 %all-to-all-done.10.gathered_ref = f32[32,24,128]{2,1,0:T(8,128)S(1)} async-done(((f32[32,24,128]{2,1,0:T(8,128)}), f32[32,24,128]{2,1,0:T(8,128)S(1)}, u32[]{:S(2)}, u32[]{:S(2)}) %all-to-all-start.10) | async-done | bytes 393248 | tf_op jit(solution)/shard_map/all_to_all | solution.py:129
  287.2 18.1 %all_to_all.91.gathered_ref = f32[32,24,128]{2,1,0:T(8,128)} all-to-all(f32[32,24,128]{2,1,0:T(8,128)S(1)} %broadcast_in_dim.45), channel_id=1, replica_groups=mesh['sec'=8,'row'=32] {'row'}, dimensions={0} | all-to-all | bytes 786432 | tf_op jit(solution)/shard_map/all_to_all | solution.py:129
  309.7 5.5 %all-to-all-start.12 = ((f32[32,24,128]{2,1,0:T(8,128)}), f32[32,24,128]{2,1,0:T(8,128)S(1)}, u32[]{:S(2)}, u32[]{:S(2)}) async-start(f32[32,24,128]{2,1,0:T(8,128)} %broadcast_in_dim.46), calls=%async_computation.12 | async-start | bytes 786432 | tf_op jit(solution)/shard_map/all_to_all | solution.py:129
  315.3 5.1 %earlier_6.1.base_ref = f32[24,128]{1,0:T(8,128)} custom-call(f32[24,128]{1,0:T(8,128)} %get-tuple-element.35.refs_0_, f32[8,2,64,2048]{3,2,1,0:T(8,128)} %bitcast.42, bf16[96,2048]{1,0:T(8,128)(2,1)} %get-tuple-element.19.refs_2_, bf16[96,2048]{1,0:T(8,128)(2,1)} %get-tuple-element.21.refs_3_, bf16[96,2048]{1,0:T(8,128)(2,1)} %get-tuple-element.23.refs_4_, ...), custom_call_target="tpu_custom_call" | custom-call | tf_op jit(solution)/shard_map/earlier_6/pallas_call | solution.py:155
  320.4 6.3 %all-to-all-done.12.gathered_ref = f32[32,24,128]{2,1,0:T(8,128)S(1)} async-done(((f32[32,24,128]{2,1,0:T(8,128)}), f32[32,24,128]{2,1,0:T(8,128)S(1)}, u32[]{:S(2)}, u32[]{:S(2)}) %all-to-all-start.12) | async-done | bytes 393248 | tf_op jit(solution)/shard_map/all_to_all | solution.py:129
  331.3 17.1 %all_to_all.92.gathered_ref = f32[32,24,128]{2,1,0:T(8,128)} all-to-all(f32[32,24,128]{2,1,0:T(8,128)S(1)} %broadcast_in_dim.47), channel_id=1, replica_groups=mesh['sec'=8,'row'=32] {'row'}, dimensions={0} | all-to-all | bytes 786432 | tf_op jit(solution)/shard_map/all_to_all | solution.py:129
  352.9 5.1 %all-to-all-start.14 = ((f32[32,24,128]{2,1,0:T(8,128)}), f32[32,24,128]{2,1,0:T(8,128)S(1)}, u32[]{:S(2)}, u32[]{:S(2)}) async-start(f32[32,24,128]{2,1,0:T(8,128)} %broadcast_in_dim.48), calls=%async_computation.14 | async-start | bytes 786432 | tf_op jit(solution)/shard_map/all_to_all | solution.py:129
  358.1 5.6 %earlier_7.1.base_ref = f32[24,128]{1,0:T(8,128)} custom-call(f32[24,128]{1,0:T(8,128)} %get-tuple-element.34.refs_0_, f32[8,2,64,2048]{3,2,1,0:T(8,128)} %bitcast.44, bf16[96,2048]{1,0:T(8,128)(2,1)} %get-tuple-element.19.refs_2_, bf16[96,2048]{1,0:T(8,128)(2,1)} %get-tuple-element.21.refs_3_, bf16[96,2048]{1,0:T(8,128)(2,1)} %get-tuple-element.23.refs_4_, ...), custom_call_target="tpu_custom_call" | custom-call | tf_op jit(solution)/shard_map/earlier_7/pallas_call | solution.py:155
  363.7 5.9 %all-to-all-done.14.gathered_ref = f32[32,24,128]{2,1,0:T(8,128)S(1)} async-done(((f32[32,24,128]{2,1,0:T(8,128)}), f32[32,24,128]{2,1,0:T(8,128)S(1)}, u32[]{:S(2)}, u32[]{:S(2)}) %all-to-all-start.14) | async-done | bytes 393248 | tf_op jit(solution)/shard_map/all_to_all | solution.py:129
  379.1 11.4 %all-to-all-done.15 = f32[32,24,128]{2,1,0:T(8,128)S(1)} async-done(((f32[32,24,128]{2,1,0:T(8,128)}), f32[32,24,128]{2,1,0:T(8,128)S(1)}, u32[]{:S(2)}, u32[]{:S(2)}) %all-to-all-start.15) | async-done | bytes 393248 | tf_op jit(solution)/shard_map/all_to_all | solution.py:129
  392.0 16.3 %all_to_all.93.packed_ref = f32[8,24,128]{2,1,0:T(8,128)} all-to-all(f32[8,24,128]{2,1,0:T(8,128)S(1)} %apply_7.1), channel_id=1, replica_groups=mesh['sec'=8,'row'=32] {'sec'}, dimensions={0} | all-to-all | bytes 196608 | tf_op jit(solution)/shard_map/all_to_all | solution.py:191
  (92 shorter events, 106.4 us)
Async XLA Ops:
  6.5 45.7 %all-gather.10.cloned.1.call-start = ((), (), s32[]{:S(2)}) async-start(), calls=%async_computation.17 | async-start | bytes 4718592 | tf_op jit(solution)/shard_map/all_gather | solution.py:120
  7.3 77.2 %all-gather.12.cloned.1.call-start = ((), (), s32[]{:S(2)}) async-start(), calls=%async_computation.18 | async-start | bytes 4718592 | tf_op jit(solution)/shard_map/all_gather | solution.py:123
  9.2 129.3 %all-gather.14.cloned.1.call-start = ((), (), s32[]{:S(2)}) async-start(), calls=%async_computation.19 | async-start | bytes 9437184 | tf_op jit(solution)/shard_map/all_gather | solution.py:123
  13.0 212.1 %all-gather.16.cloned.1.call-start = ((), (), s32[]{:S(2)}) async-start(), calls=%async_computation.20 | async-start | bytes 9437184 | tf_op jit(solution)/shard_map/all_gather | solution.py:123
  13.6 301.7 %all-gather.18.cloned.1.call-start = ((), (), s32[]{:S(2)}) async-start(), calls=%async_computation.21 | async-start | bytes 9437184 | tf_op jit(solution)/shard_map/all_gather | solution.py:123
  56.8 27.7 %all-to-all-start.2 = ((f32[32,24,128]{2,1,0:T(8,128)}), f32[32,24,128]{2,1,0:T(8,128)S(1)}, u32[]{:S(2)}, u32[]{:S(2)}) async-start(f32[32,24,128]{2,1,0:T(8,128)} %broadcast_in_dim.36), calls=%async_computation.2 | async-start | bytes 786432 | tf_op jit(solution)/shard_map/all_to_all | solution.py:129
  117.1 24.5 %all-to-all-start.4 = ((f32[32,24,128]{2,1,0:T(8,128)}), f32[32,24,128]{2,1,0:T(8,128)S(1)}, u32[]{:S(2)}, u32[]{:S(2)}) async-start(f32[32,24,128]{2,1,0:T(8,128)} %broadcast_in_dim.38), calls=%async_computation.4 | async-start | bytes 786432 | tf_op jit(solution)/shard_map/all_to_all | solution.py:129
  174.2 17.6 %all-to-all-start.6 = ((f32[32,24,128]{2,1,0:T(8,128)}), f32[32,24,128]{2,1,0:T(8,128)S(1)}, u32[]{:S(2)}, u32[]{:S(2)}) async-start(f32[32,24,128]{2,1,0:T(8,128)} %broadcast_in_dim.40), calls=%async_computation.6 | async-start | bytes 786432 | tf_op jit(solution)/shard_map/all_to_all | solution.py:129
  191.9 0.8 copy-start.4
  219.3 18.4 %all-to-all-start.8 = ((f32[32,24,128]{2,1,0:T(8,128)}), f32[32,24,128]{2,1,0:T(8,128)S(1)}, u32[]{:S(2)}, u32[]{:S(2)}) async-start(f32[32,24,128]{2,1,0:T(8,128)} %broadcast_in_dim.42), calls=%async_computation.8 | async-start | bytes 786432 | tf_op jit(solution)/shard_map/all_to_all | solution.py:129
  237.7 0.8 copy-start.2
  265.1 17.6 %all-to-all-start.10 = ((f32[32,24,128]{2,1,0:T(8,128)}), f32[32,24,128]{2,1,0:T(8,128)S(1)}, u32[]{:S(2)}, u32[]{:S(2)}) async-start(f32[32,24,128]{2,1,0:T(8,128)} %broadcast_in_dim.44), calls=%async_computation.10 | async-start | bytes 786432 | tf_op jit(solution)/shard_map/all_to_all | solution.py:129
  282.6 0.8 copy-start.5
  309.7 17.0 %all-to-all-start.12 = ((f32[32,24,128]{2,1,0:T(8,128)}), f32[32,24,128]{2,1,0:T(8,128)S(1)}, u32[]{:S(2)}, u32[]{:S(2)}) async-start(f32[32,24,128]{2,1,0:T(8,128)} %broadcast_in_dim.46), calls=%async_computation.12 | async-start | bytes 786432 | tf_op jit(solution)/shard_map/all_to_all | solution.py:129
  330.5 27.5 %copy-start.7 = (f32[24,128]{1,0:T(8,128)S(1)}, f32[24,128]{1,0:T(8,128)}, u32[]{:S(2)}) copy-start(f32[24,128]{1,0:T(8,128)} %apply_0.1) | copy-start | bytes 36868
  330.5 27.5 %copy-start.8 = (f32[24,128]{1,0:T(8,128)S(1)}, f32[24,128]{1,0:T(8,128)}, u32[]{:S(2)}) copy-start(f32[24,128]{1,0:T(8,128)} %apply_1.1) | copy-start | bytes 36868
  330.5 27.5 %copy-start.10 = (f32[24,128]{1,0:T(8,128)S(1)}, f32[24,128]{1,0:T(8,128)}, u32[]{:S(2)}) copy-start(f32[24,128]{1,0:T(8,128)} %apply_2.1) | copy-start | bytes 36868
  352.9 16.6 %all-to-all-start.14 = ((f32[32,24,128]{2,1,0:T(8,128)}), f32[32,24,128]{2,1,0:T(8,128)S(1)}, u32[]{:S(2)}, u32[]{:S(2)}) async-start(f32[32,24,128]{2,1,0:T(8,128)} %broadcast_in_dim.48), calls=%async_computation.14 | async-start | bytes 786432 | tf_op jit(solution)/shard_map/all_to_all | solution.py:129
  363.7 15.3 %copy-start.9 = (f32[24,128]{1,0:T(8,128)S(1)}, f32[24,128]{1,0:T(8,128)}, u32[]{:S(2)}) copy-start(f32[24,128]{1,0:T(8,128)} %apply_3.1) | copy-start | bytes 36868
  363.7 15.3 %copy-start.11 = (f32[24,128]{1,0:T(8,128)S(1)}, f32[24,128]{1,0:T(8,128)}, u32[]{:S(2)}) copy-start(f32[24,128]{1,0:T(8,128)} %apply_4.1) | copy-start | bytes 36868
  363.7 15.3 %copy-start.12 = (f32[24,128]{1,0:T(8,128)S(1)}, f32[24,128]{1,0:T(8,128)}, u32[]{:S(2)}) copy-start(f32[24,128]{1,0:T(8,128)} %apply_5.1) | copy-start | bytes 36868
  363.7 15.3 %copy-start.13 = (f32[24,128]{1,0:T(8,128)S(1)}, f32[24,128]{1,0:T(8,128)}, u32[]{:S(2)}) copy-start(f32[24,128]{1,0:T(8,128)} %apply_6.1) | copy-start | bytes 36868
  369.6 0.8 copy-start
  374.9 15.6 %all-to-all-start.15 = ((f32[32,24,128]{2,1,0:T(8,128)}), f32[32,24,128]{2,1,0:T(8,128)S(1)}, u32[]{:S(2)}, u32[]{:S(2)}) async-start(f32[32,24,128]{2,1,0:T(8,128)} %broadcast_in_dim.49), calls=%async_computation.15 | async-start | bytes 786432 | tf_op jit(solution)/shard_map/all_to_all | solution.py:129
  (3 other events, 2.3 us)
Sparse Core Ops, SparseCore 0:
  9.2 38.7 all-gather.9
  49.8 34.5 all-gather.11
  86.3 52.1 all-gather.13
  140.3 52.3 all-gather.15
  194.4 52.4 all-gather.17

commit v2 on v1

v2 whole, which is shorter than its diff:
```python
import functools

import jax
import jax.numpy as jnp
from jax import lax
from jax.experimental import pallas as pl
from jax.experimental.pallas import tpu as pltpu
from jax.sharding import PartitionSpec as P

LANES = 128
VMEM = pl.BlockSpec(memory_space=pltpu.VMEM)
HBM = pl.BlockSpec(memory_space=pltpu.HBM)


def low_lanes(shape):
    return lax.broadcasted_iota(jnp.int32, shape, 1) < LANES // 2


def pack_kernel(rhs_ref, out_ref):
    groups, half, _ = out_ref.shape
    rows = rhs_ref[...]
    turned = jnp.concatenate([rows, rows], axis=0).T
    low = low_lanes((half, LANES))
    for group in range(groups):
        start = 2 * group * half
        top = turned[start : start + half]
        bottom = turned[start + half : start + 2 * half]
        out_ref[group] = jnp.where(low, top, bottom)


def unpack_kernel(packed_ref, out_ref):
    groups = packed_ref.shape[0]
    pieces = []
    for group in range(groups):
        tile = packed_ref[group]
        pieces += [tile, pltpu.roll(tile, LANES // 2, 1)]
    turned = jnp.concatenate(pieces, axis=0).T
    out_ref[...] = turned[: LANES // 2]


def split(values):
    high = values.astype(jnp.bfloat16)
    low = (values - high.astype(jnp.float32)).astype(jnp.bfloat16)
    return high, low


def spread(gathered_ref, whole_ref, parts_ref):
    devices, half, _ = gathered_ref.shape
    low = low_lanes((half, LANES))
    for pair in range(devices // 2):
        first = gathered_ref[2 * pair]
        second = gathered_ref[2 * pair + 1]
        lanes = slice(pair * LANES, (pair + 1) * LANES)
        whole_ref[:half, lanes] = jnp.where(low, first, pltpu.roll(second, LANES // 2, 1))
        whole_ref[half:, lanes] = jnp.where(low, pltpu.roll(first, LANES // 2, 1), second)
    high, rest = split(whole_ref[...])
    parts_ref[: 2 * half] = high
    parts_ref[2 * half :] = rest


def times(parts, matrix):
    cols = parts.shape[0] // 2
    high, low = split(matrix)
    dims = (((1,), (1,)), ((), ()))
    both = lax.dot_general(parts, high, dims, preferred_element_type=jnp.float32)
    rest = lax.dot_general(parts[:cols], low, dims, preferred_element_type=jnp.float32)
    return both[:cols] + (both[cols:] + rest)


def packed(turned):
    half = turned.shape[0] // 2
    return jnp.concatenate([turned[:half], turned[half:]], axis=1)


def fetch_kernel(index, matrix_ref, out_ref, sem):
    copy = pltpu.make_async_copy(matrix_ref.at[index], out_ref, sem)
    copy.start()
    copy.wait()


def apply_kernel(gathered_ref, matrix_ref, tile_ref, copies_ref, whole, parts):
    spread(gathered_ref, whole, parts)
    tile = packed(times(parts[...], matrix_ref[...]))
    tile_ref[...] = tile
    copies_ref[...] = jnp.broadcast_to(tile[None], copies_ref.shape)


def last_kernel(gathered_ref, matrix_ref, tile_ref, whole, parts):
    spread(gathered_ref, whole, parts)
    tile_ref[...] = packed(times(parts[...], matrix_ref[...]))


def residual_kernel(gathered_ref, base_ref, matrix_ref, copies_ref, parts, whole):
    spread(gathered_ref, whole, parts)
    tile = base_ref[...] - packed(times(parts[...], matrix_ref[...]))
    copies_ref[...] = jnp.broadcast_to(tile[None], copies_ref.shape)


def earlier_kernel(places, follow, *refs):
    count = len(places)
    base_ref, inverses_ref = refs[:2]
    panels = refs[2 : 2 + len(follow[1])]
    parts_refs = refs[2 + len(panels) : 2 + len(panels) + count - 1]
    base_out, matrix_out, inverse_out, blocks, sems = refs[2 + len(panels) + count - 1 :]
    targets = [blocks.at[k] for k in range(count - 1)] + [matrix_out]
    copies = []
    for k, (panel, slot) in enumerate(places):
        copies.append(pltpu.make_async_copy(panels[panel].at[slot], targets[k], sems.at[k]))
    copies.append(pltpu.make_async_copy(inverses_ref.at[follow[0]], inverse_out, sems.at[count]))
    for copy in copies:
        copy.start()
    total = base_ref[...]
    for k in range(count - 1):
        copies[k].wait()
        total = total - packed(times(parts_refs[k][...], blocks[k]))
    base_out[...] = total
    copies[count - 1].wait()
    copies[count].wait()


def in_vmem(value):
    return pltpu.with_memory_space_constraint(value, pltpu.VMEM)


def in_hbm(value):
    return pltpu.with_memory_space_constraint(value, pltpu.HBM)


def shards(factor, inverse_blocks, right_side):
    sections = lax.axis_size("sec")
    segment = lax.axis_index("sec")
    lines = lax.axis_size("row")
    local_rows, block = factor.shape[1:]
    cols = right_side.shape[2] // sections
    half = cols // 2
    f32 = jnp.float32
    tile = jax.ShapeDtypeStruct((half, LANES), f32)
    tile_in_vmem = pltpu.VMEM((half, LANES), f32)
    copies_in_vmem = pltpu.VMEM((lines, half, LANES), f32)
    parts_in_vmem = pltpu.VMEM((2 * cols, block), jnp.bfloat16)
    matrix_in_vmem = pltpu.VMEM((local_rows, block), f32)
    whole_scratch = pltpu.VMEM((cols, block), f32)
    params = pltpu.CompilerParams(vmem_limit_bytes=24 << 20)

    chunks = pl.pallas_call(
        pack_kernel,
        out_shape=jax.ShapeDtypeStruct((sections, half, LANES), f32),
        in_specs=[VMEM],
        out_specs=VMEM,
        compiler_params=params,
        name="pack",
    )(right_side[0])
    given = lax.all_to_all(chunks, "sec", 0, 0, tiled=True)

    inverses = lax.all_gather(inverse_blocks[0], "sec", axis=0)

    middle = sections // 2

    def panel(factor, d):
        far = {1: sections, middle: sections - 1}.get(d, sections - d)
        own = lax.dynamic_index_in_dim(factor, jnp.minimum(segment + d, sections - 1), 0, False)
        if far < sections:
            sent = lax.dynamic_index_in_dim(
                factor, jnp.minimum(segment + far, sections - 1), 0, False
            )
            route = [(k, k + far) for k in range(sections - far)]
            moved = lax.ppermute(sent, "sec", route)
            own = jnp.where(segment + d < sections, own, moved)
        return lax.all_gather(own, "sec", axis=0)

    def place(j, k):
        d = j - k
        if d <= middle:
            return d, k
        return (middle if d + 1 == sections else sections - d), j

    panels = {1: panel(factor, 1)}

    def exchange(copies):
        return lax.all_to_all(copies, "row", 0, 0, tiled=True)

    def fetch(i):
        return pl.pallas_call(
            functools.partial(fetch_kernel, i),
            out_shape=matrix_in_vmem,
            in_specs=[HBM],
            out_specs=VMEM,
            scratch_shapes=[pltpu.SemaphoreType.DMA],
            compiler_params=params,
            name=f"fetch_{i}",
        )(in_hbm(inverses))

    def apply(i, gathered, inverse):
        last = i + 1 == sections
        return pl.pallas_call(
            last_kernel if last else apply_kernel,
            out_shape=tile if last else (tile, copies_in_vmem),
            in_specs=[VMEM, VMEM],
            out_specs=VMEM if last else (VMEM, VMEM),
            scratch_shapes=[whole_scratch, parts_in_vmem],
            compiler_params=params,
            name=f"apply_{i}",
        )(in_vmem(gathered), in_vmem(inverse))

    def residual(j, gathered, base, matrix):
        return pl.pallas_call(
            residual_kernel,
            out_shape=(copies_in_vmem, parts_in_vmem),
            in_specs=[VMEM, VMEM, VMEM],
            out_specs=(VMEM, VMEM),
            scratch_shapes=[whole_scratch],
            compiler_params=params,
            name=f"residual_{j}",
        )(in_vmem(gathered), in_vmem(base), in_vmem(matrix))

    def earlier(j, base, known):
        where = [place(j, k) for k in range(j)]
        used = sorted({d for d, _ in where})
        places = [(used.index(d), slot) for d, slot in where]
        return pl.pallas_call(
            functools.partial(earlier_kernel, places, (j, used)),
            out_shape=(tile_in_vmem, matrix_in_vmem, matrix_in_vmem),
            in_specs=[VMEM, HBM] + [HBM] * len(used) + [VMEM] * len(known),
            out_specs=(VMEM, VMEM, VMEM),
            scratch_shapes=[
                pltpu.VMEM((max(j - 1, 1), local_rows, block), f32),
                pltpu.SemaphoreType.DMA((j + 1,)),
            ],
            compiler_params=params,
            name=f"earlier_{j}",
        )(
            base,
            in_hbm(inverses),
            *[in_hbm(panels[d]) for d in used],
            *[in_vmem(parts) for parts in known],
        )

    pieces = []
    known = []
    copies = jnp.broadcast_to(given[0][None], (lines, half, LANES))
    inverse = fetch(0)
    for i in range(sections):
        gathered = exchange(copies)
        if i == 0:
            gathered, factor = lax.optimization_barrier((gathered, factor))
            panels |= {d: panel(factor, d) for d in range(2, middle + 1)}
        if i + 1 == sections:
            pieces.append(apply(i, gathered, inverse))
            break
        piece, copies = apply(i, gathered, inverse)
        pieces.append(piece)
        gathered = exchange(copies)
        base, matrix, inverse = earlier(i + 1, given[i + 1], known)
        copies, parts = residual(i + 1, gathered, base, matrix)
        known.append(parts)

    found = lax.all_to_all(jnp.stack(pieces), "sec", 0, 0, tiled=True)
    out = pl.pallas_call(
        unpack_kernel,
        out_shape=jax.ShapeDtypeStruct(right_side.shape[1:], f32),
        in_specs=[VMEM],
        out_specs=VMEM,
        compiler_params=params,
        name="unpack",
    )(found)
    return out[None]


def solution(mesh):
    return jax.shard_map(
        shards,
        mesh=mesh,
        in_specs=(P(None, "row", "sec"), P("sec", "row", None), P("sec", "row", None)),
        out_specs=P("sec", "row", None),
        check_vma=False,
    )
```

time: 420 us -> 389 us (0.926)
  waiting for transfers between devices: 89.3 us -> 134 us
  Pallas kernels: 72 us -> 33.3 us
  blocking collectives: 171 us -> 133 us
  starting transfers between devices: 41.2 us -> 60.7 us
  local copies, waits for them, and re-layouts: 29.5 us -> 10.2 us
    all_to_all x8 -> x9, waiting for transfers between devices: 48.4 us -> 90.8 us  [exchange(): return lax.all_to_all(copies, 'row', 0, 0, tiled=True)]
    ppermute x0 -> x3, waiting for transfers between devices: none -> 41.2 us  [panel(): moved = lax.ppermute(sent, 'sec', route)]
    all_gather x4, waiting for transfers between devices: 39.1 us -> 0.08 us  [panel(): return lax.all_gather(own, 'sec', axis=0)]
    pallas_call x20 -> x22, Pallas kernels: 68.6 us -> 32.4 us  [the longest x7 18.8 us: earlier(): pl.pallas_call(functools.partial(earlier_kernel, places, (j, used)), out_...]
    all_to_all x7 -> x6, blocking collectives: 143 us -> 108 us  [exchange(): return lax.all_to_all(copies, 'row', 0, 0, tiled=True)]
    broadcast_in_dim x15 -> x1, local copies, waits for them, and re-layouts: 16.4 us -> 0.77 us  [shards(): copies = jnp.broadcast_to(given[0][None], (lines, half, LANES))]
    all_to_all x8 -> x9, starting transfers between devices: 41 us -> 52.4 us  [exchange(): return lax.all_to_all(copies, 'row', 0, 0, tiled=True)]
    ppermute x0 -> x3, starting transfers between devices: none -> 8.09 us  [panel(): moved = lax.ppermute(sent, 'sec', route)]
  transfers between devices with their start and end apart: 13 -> 17, of which waited for: 8 -> 11; matrix products, arithmetic and copies ran while one was open for 5% -> 2% of each run, Pallas kernels for 15% -> 7%
where the time goes in v2:
time: 389 us; the launch traced here: 387 us
  waiting for transfers between devices  134 us (34%)
  blocking collectives  133 us (34%)
  starting transfers between devices  60.7 us (16%)
  Pallas kernels  33.3 us (9%)
  between operations  13.5 us (3%)
  local copies, waits for them, and re-layouts  10.2 us (3%)
    all_to_all x6, blocking collectives, exchange(): return lax.all_to_all(copies, 'row', 0, 0, tiled=True)  108 us
    all_to_all x9, waiting for transfers between devices, exchange(): return lax.all_to_all(copies, 'row', 0, 0, tiled=True)  90.8 us
    all_to_all x9, starting transfers between devices, exchange(): return lax.all_to_all(copies, 'row', 0, 0, tiled=True)  52.4 us
    ppermute x3, waiting for transfers between devices, panel(): moved = lax.ppermute(sent, 'sec', route)  41.2 us
    pallas_call x7, Pallas kernels, earlier(): pl.pallas_call(functools.partial(earlier_kernel, places, (j, used)), out_...  18.8 us
    all_to_all x1, blocking collectives, shards(): found = lax.all_to_all(jnp.stack(pieces), 'sec', 0, 0, tiled=True)  14.7 us
    all_to_all x1, blocking collectives, shards(): given = lax.all_to_all(chunks, 'sec', 0, 0, tiled=True)  10.6 us
    pallas_call x7, Pallas kernels, apply(): pl.pallas_call(last_kernel if last else apply_kernel, out_shape=tile if l...  8.49 us
  transfers between devices with their start and end apart: 17, of which 11 were waited for; matrix products, arithmetic and copies ran while one was open for 2% of the time, Pallas kernels for 7%

profile of v2, /device:TPU:1, one launch (start us, length us, event | category | flops | bytes accessed | tf_op | source)
XLA Modules:
  0.0 387.2 jit_solution(13922931515025566179)
XLA Ops:
  10.3 10.6 %all_to_all.85 = f32[8,24,128]{2,1,0:T(8,128)S(1)} all-to-all(f32[8,24,128]{2,1,0:T(8,128)S(1)} %pack.1), channel_id=1, replica_groups=mesh['sec'=8,'row'=32] {'sec'}, dimensions={0} | all-to-all | bytes 196608 | tf_op jit(solution)/shard_map/all_to_all | solution.py:153
  21.6 11.2 %all-to-all-start.1 = ((f32[32,24,128]{2,1,0:T(8,128)}), f32[32,24,128]{2,1,0:T(8,128)S(1)}, u32[]{:S(2)}, u32[]{:S(2)}) async-start(f32[32,24,128]{2,1,0:T(8,128)} %broadcast_in_dim.11), calls=%async_computation.1 | async-start | bytes 786432 | tf_op jit(solution)/shard_map/all_to_all | solution.py:180
  32.9 13.9 %all-to-all-done.1.gathered_ref = f32[32,24,128]{2,1,0:T(8,128)S(1)} async-done(((f32[32,24,128]{2,1,0:T(8,128)}), f32[32,24,128]{2,1,0:T(8,128)S(1)}, u32[]{:S(2)}, u32[]{:S(2)}) %all-to-all-start.1) | async-done | bytes 393248 | tf_op jit(solution)/shard_map/all_to_all | solution.py:180
  56.4 22.3 %collective-permute-done.1 = f32[64,2048]{1,0:T(8,128)S(1)} collective-permute-done((f32[64,2048]{1,0:T(8,128)S(1)}, f32[64,2048]{1,0:T(8,128)S(1)}, u32[]{:S(2)}, u32[]{:S(2)}) %collective-permute-start.1) | collective-permute-done | bytes 524320 | tf_op jit(solution)/shard_map/ppermute | solution.py:167
  78.7 18.9 %collective-permute-done = f32[64,2048]{1,0:T(8,128)} collective-permute-done((f32[64,2048]{1,0:T(8,128)S(1)}, f32[64,2048]{1,0:T(8,128)}, u32[]{:S(2)}, u32[]{:S(2)}) %collective-permute-start) | collective-permute-done | bytes 524320 | tf_op jit(solution)/shard_map/ppermute | solution.py:167
  108.8 13.1 %all-to-all-done.2.gathered_ref = f32[32,24,128]{2,1,0:T(8,128)S(1)} async-done(((f32[32,24,128]{2,1,0:T(8,128)}), f32[32,24,128]{2,1,0:T(8,128)S(1)}, u32[]{:S(2)}, u32[]{:S(2)}) %all-to-all-start.2) | async-done | bytes 393248 | tf_op jit(solution)/shard_map/all_to_all | solution.py:180
  122.4 19.1 %all_to_all.86.gathered_ref = f32[32,24,128]{2,1,0:T(8,128)S(1)} all-to-all(f32[32,24,128]{2,1,0:T(8,128)S(1)} %get-tuple-element.60), channel_id=1, replica_groups=mesh['sec'=8,'row'=32] {'row'}, dimensions={0} | all-to-all | bytes 786432 | tf_op jit(solution)/shard_map/all_to_all | solution.py:180
  148.6 12.0 %all-to-all-done.4.gathered_ref = f32[32,24,128]{2,1,0:T(8,128)S(1)} async-done(((f32[32,24,128]{2,1,0:T(8,128)}), f32[32,24,128]{2,1,0:T(8,128)S(1)}, u32[]{:S(2)}, u32[]{:S(2)}) %all-to-all-start.4) | async-done | bytes 393248 | tf_op jit(solution)/shard_map/all_to_all | solution.py:180
  161.1 17.6 %all_to_all.87.gathered_ref = f32[32,24,128]{2,1,0:T(8,128)S(1)} all-to-all(f32[32,24,128]{2,1,0:T(8,128)S(1)} %get-tuple-element.68), channel_id=1, replica_groups=mesh['sec'=8,'row'=32] {'row'}, dimensions={0} | all-to-all | bytes 786432 | tf_op jit(solution)/shard_map/all_to_all | solution.py:180
  179.9 5.8 %all-to-all-start.6 = ((f32[32,24,128]{2,1,0:T(8,128)}), f32[32,24,128]{2,1,0:T(8,128)S(1)}, u32[]{:S(2)}, u32[]{:S(2)}) async-start(f32[32,24,128]{2,1,0:T(8,128)} %get-tuple-element.71), calls=%async_computation.6 | async-start | bytes 786432 | tf_op jit(solution)/shard_map/all_to_all | solution.py:180
  187.9 10.7 %all-to-all-done.6.gathered_ref = f32[32,24,128]{2,1,0:T(8,128)S(1)} async-done(((f32[32,24,128]{2,1,0:T(8,128)}), f32[32,24,128]{2,1,0:T(8,128)S(1)}, u32[]{:S(2)}, u32[]{:S(2)}) %all-to-all-start.6) | async-done | bytes 393248 | tf_op jit(solution)/shard_map/all_to_all | solution.py:180
  199.1 18.0 %all_to_all.88.gathered_ref = f32[32,24,128]{2,1,0:T(8,128)S(1)} all-to-all(f32[32,24,128]{2,1,0:T(8,128)S(1)} %get-tuple-element.75), channel_id=1, replica_groups=mesh['sec'=8,'row'=32] {'row'}, dimensions={0} | all-to-all | bytes 786432 | tf_op jit(solution)/shard_map/all_to_all | solution.py:180
  218.3 5.8 %all-to-all-start.8 = ((f32[32,24,128]{2,1,0:T(8,128)}), f32[32,24,128]{2,1,0:T(8,128)S(1)}, u32[]{:S(2)}, u32[]{:S(2)}) async-start(f32[32,24,128]{2,1,0:T(8,128)} %get-tuple-element.78), calls=%async_computation.8 | async-start | bytes 786432 | tf_op jit(solution)/shard_map/all_to_all | solution.py:180
  226.7 10.0 %all-to-all-done.8.gathered_ref = f32[32,24,128]{2,1,0:T(8,128)S(1)} async-done(((f32[32,24,128]{2,1,0:T(8,128)}), f32[32,24,128]{2,1,0:T(8,128)S(1)}, u32[]{:S(2)}, u32[]{:S(2)}) %all-to-all-start.8) | async-done | bytes 393248 | tf_op jit(solution)/shard_map/all_to_all | solution.py:180
  237.2 18.2 %all_to_all.89.gathered_ref = f32[32,24,128]{2,1,0:T(8,128)S(1)} all-to-all(f32[32,24,128]{2,1,0:T(8,128)S(1)} %get-tuple-element.82), channel_id=1, replica_groups=mesh['sec'=8,'row'=32] {'row'}, dimensions={0} | all-to-all | bytes 786432 | tf_op jit(solution)/shard_map/all_to_all | solution.py:180
  256.5 5.7 %all-to-all-start.10 = ((f32[32,24,128]{2,1,0:T(8,128)}), f32[32,24,128]{2,1,0:T(8,128)S(1)}, u32[]{:S(2)}, u32[]{:S(2)}) async-start(f32[32,24,128]{2,1,0:T(8,128)} %get-tuple-element.85), calls=%async_computation.10 | async-start | bytes 786432 | tf_op jit(solution)/shard_map/all_to_all | solution.py:180
  265.5 8.6 %all-to-all-done.10.gathered_ref = f32[32,24,128]{2,1,0:T(8,128)S(1)} async-done(((f32[32,24,128]{2,1,0:T(8,128)}), f32[32,24,128]{2,1,0:T(8,128)S(1)}, u32[]{:S(2)}, u32[]{:S(2)}) %all-to-all-start.10) | async-done | bytes 393248 | tf_op jit(solution)/shard_map/all_to_all | solution.py:180
  274.6 18.0 %all_to_all.90.gathered_ref = f32[32,24,128]{2,1,0:T(8,128)S(1)} all-to-all(f32[32,24,128]{2,1,0:T(8,128)S(1)} %get-tuple-element.89), channel_id=1, replica_groups=mesh['sec'=8,'row'=32] {'row'}, dimensions={0} | all-to-all | bytes 786432 | tf_op jit(solution)/shard_map/all_to_all | solution.py:180
  293.7 5.9 %all-to-all-start.12 = ((f32[32,24,128]{2,1,0:T(8,128)}), f32[32,24,128]{2,1,0:T(8,128)S(1)}, u32[]{:S(2)}, u32[]{:S(2)}) async-start(f32[32,24,128]{2,1,0:T(8,128)} %get-tuple-element.92), calls=%async_computation.12 | async-start | bytes 786432 | tf_op jit(solution)/shard_map/all_to_all | solution.py:180
  303.3 8.0 %all-to-all-done.12.gathered_ref = f32[32,24,128]{2,1,0:T(8,128)S(1)} async-done(((f32[32,24,128]{2,1,0:T(8,128)}), f32[32,24,128]{2,1,0:T(8,128)S(1)}, u32[]{:S(2)}, u32[]{:S(2)}) %all-to-all-start.12) | async-done | bytes 393248 | tf_op jit(solution)/shard_map/all_to_all | solution.py:180
  311.8 16.9 %all_to_all.91.gathered_ref = f32[32,24,128]{2,1,0:T(8,128)S(1)} all-to-all(f32[32,24,128]{2,1,0:T(8,128)S(1)} %get-tuple-element.96), channel_id=1, replica_groups=mesh['sec'=8,'row'=32] {'row'}, dimensions={0} | all-to-all | bytes 786432 | tf_op jit(solution)/shard_map/all_to_all | solution.py:180
  330.0 5.6 %all-to-all-start.14 = ((f32[32,24,128]{2,1,0:T(8,128)}), f32[32,24,128]{2,1,0:T(8,128)S(1)}, u32[]{:S(2)}, u32[]{:S(2)}) async-start(f32[32,24,128]{2,1,0:T(8,128)} %get-tuple-element.99), calls=%async_computation.14 | async-start | bytes 786432 | tf_op jit(solution)/shard_map/all_to_all | solution.py:180
  355.1 9.0 %all-to-all-done.15 = f32[32,24,128]{2,1,0:T(8,128)S(1)} async-done(((f32[32,24,128]{2,1,0:T(8,128)}), f32[32,24,128]{2,1,0:T(8,128)S(1)}, u32[]{:S(2)}, u32[]{:S(2)}) %all-to-all-start.15) | async-done | bytes 393248 | tf_op jit(solution)/shard_map/all_to_all | solution.py:180
  365.2 14.7 %all_to_all.92.packed_ref = f32[8,24,128]{2,1,0:T(8,128)S(1)} all-to-all(f32[8,24,128]{2,1,0:T(8,128)} %apply_7.1), channel_id=1, replica_groups=mesh['sec'=8,'row'=32] {'sec'}, dimensions={0} | all-to-all | bytes 196608 | tf_op jit(solution)/shard_map/all_to_all | solution.py:257
  (68 shorter events, 74.1 us)
Async XLA Ops:
  6.5 94.8 %all-gather.9.cloned.1.call-start = ((), (), s32[]{:S(2)}) async-start(), calls=%async_computation.17 | async-start | bytes 4718592 | tf_op jit(solution)/shard_map/all_gather | solution.py:155
  7.3 100.3 %all-gather.11.cloned.1.call-start = ((), (), s32[]{:S(2)}) async-start(), calls=%async_computation.18 | async-start | bytes 4718592 | tf_op jit(solution)/shard_map/all_gather | solution.py:169
  9.2 0.9 copy-start.2
  21.6 25.1 %all-to-all-start.1 = ((f32[32,24,128]{2,1,0:T(8,128)}), f32[32,24,128]{2,1,0:T(8,128)S(1)}, u32[]{:S(2)}, u32[]{:S(2)}) async-start(f32[32,24,128]{2,1,0:T(8,128)} %broadcast_in_dim.11), calls=%async_computation.1 | async-start | bytes 786432 | tf_op jit(solution)/shard_map/all_to_all | solution.py:180
  32.8 114.0 %all-gather.13.cloned.1.call-start = ((), (), s32[]{:S(2)}) async-start(), calls=%async_computation.19 | async-start | bytes 4718592 | tf_op jit(solution)/shard_map/all_gather | solution.py:169
  48.3 8.1 %collective-permute-start.2 = (f32[64,2048]{1,0:T(8,128)S(1)}, f32[64,2048]{1,0:T(8,128)S(1)}, u32[]{:S(2)}, u32[]{:S(2)}) collective-permute-start(f32[64,2048]{1,0:T(8,128)S(1)} %get-tuple-element.108), channel_id=1, source_target_pairs={{0,224},{1,225},{2,226},{3,227},{4,228},{5,229},{6,230},{7,231},{8... | collective-permute-start | bytes 1572872 | tf_op jit(solution)/shard_map/ppermute | solution.py:167
  49.0 29.7 %collective-permute-start.1 = (f32[64,2048]{1,0:T(8,128)S(1)}, f32[64,2048]{1,0:T(8,128)S(1)}, u32[]{:S(2)}, u32[]{:S(2)}) collective-permute-start(f32[64,2048]{1,0:T(8,128)S(1)} %get-tuple-element.109), channel_id=1, source_target_pairs={{0,160},{32,192},{64,224},{1,161},{33,193},{65,225},{2,162},{34,19... | collective-permute-start | bytes 1572872 | tf_op jit(solution)/shard_map/ppermute | solution.py:167
  54.3 43.3 %collective-permute-start = (f32[64,2048]{1,0:T(8,128)S(1)}, f32[64,2048]{1,0:T(8,128)}, u32[]{:S(2)}, u32[]{:S(2)}) collective-permute-start(f32[64,2048]{1,0:T(8,128)S(1)} %get-tuple-element.110), channel_id=1, source_target_pairs={{0,192},{32,224},{1,193},{33,225},{2,194},{34,226},{3,195},{35,227... | collective-permute-start | bytes 1572872 | tf_op jit(solution)/shard_map/ppermute | solution.py:167
  100.2 85.6 %all-gather.15.cloned.1.call-start = ((), (), s32[]{:S(2)}) async-start(), calls=%async_computation.20 | async-start | bytes 4718592 | tf_op jit(solution)/shard_map/all_gather | solution.py:169
  100.8 123.4 %all-gather.17.cloned.1.call-start = ((), (), s32[]{:S(2)}) async-start(), calls=%async_computation.21 | async-start | bytes 4718592 | tf_op jit(solution)/shard_map/all_gather | solution.py:169
  103.7 18.3 %all-to-all-start.2 = ((f32[32,24,128]{2,1,0:T(8,128)}), f32[32,24,128]{2,1,0:T(8,128)S(1)}, u32[]{:S(2)}, u32[]{:S(2)}) async-start(f32[32,24,128]{2,1,0:T(8,128)} %get-tuple-element.57), calls=%async_computation.2 | async-start | bytes 786432 | tf_op jit(solution)/shard_map/all_to_all | solution.py:180
  142.7 17.8 %all-to-all-start.4 = ((f32[32,24,128]{2,1,0:T(8,128)}), f32[32,24,128]{2,1,0:T(8,128)S(1)}, u32[]{:S(2)}, u32[]{:S(2)}) async-start(f32[32,24,128]{2,1,0:T(8,128)} %get-tuple-element.63), calls=%async_computation.4 | async-start | bytes 786432 | tf_op jit(solution)/shard_map/all_to_all | solution.py:180
  179.9 18.7 %all-to-all-start.6 = ((f32[32,24,128]{2,1,0:T(8,128)}), f32[32,24,128]{2,1,0:T(8,128)S(1)}, u32[]{:S(2)}, u32[]{:S(2)}) async-start(f32[32,24,128]{2,1,0:T(8,128)} %get-tuple-element.71), calls=%async_computation.6 | async-start | bytes 786432 | tf_op jit(solution)/shard_map/all_to_all | solution.py:180
  218.3 18.4 %all-to-all-start.8 = ((f32[32,24,128]{2,1,0:T(8,128)}), f32[32,24,128]{2,1,0:T(8,128)S(1)}, u32[]{:S(2)}, u32[]{:S(2)}) async-start(f32[32,24,128]{2,1,0:T(8,128)} %get-tuple-element.78), calls=%async_computation.8 | async-start | bytes 786432 | tf_op jit(solution)/shard_map/all_to_all | solution.py:180
  256.5 17.5 %all-to-all-start.10 = ((f32[32,24,128]{2,1,0:T(8,128)}), f32[32,24,128]{2,1,0:T(8,128)S(1)}, u32[]{:S(2)}, u32[]{:S(2)}) async-start(f32[32,24,128]{2,1,0:T(8,128)} %get-tuple-element.85), calls=%async_computation.10 | async-start | bytes 786432 | tf_op jit(solution)/shard_map/all_to_all | solution.py:180
  293.7 17.6 %all-to-all-start.12 = ((f32[32,24,128]{2,1,0:T(8,128)}), f32[32,24,128]{2,1,0:T(8,128)S(1)}, u32[]{:S(2)}, u32[]{:S(2)}) async-start(f32[32,24,128]{2,1,0:T(8,128)} %get-tuple-element.92), calls=%async_computation.12 | async-start | bytes 786432 | tf_op jit(solution)/shard_map/all_to_all | solution.py:180
  311.8 18.1 %copy-start = (bf16[96,2048]{1,0:T(8,128)(2,1)}, bf16[96,2048]{1,0:T(8,128)(2,1)S(1)}, u32[]{:S(2)}) copy-start(bf16[96,2048]{1,0:T(8,128)(2,1)S(1)} %get-tuple-element.100.refs_11_) | copy-start | bytes 1179652
  330.0 17.1 %all-to-all-start.14 = ((f32[32,24,128]{2,1,0:T(8,128)}), f32[32,24,128]{2,1,0:T(8,128)S(1)}, u32[]{:S(2)}, u32[]{:S(2)}) async-start(f32[32,24,128]{2,1,0:T(8,128)} %get-tuple-element.99), calls=%async_computation.14 | async-start | bytes 786432 | tf_op jit(solution)/shard_map/all_to_all | solution.py:180
  335.6 0.6 copy-start.3
  336.3 1.0 copy-start.1
  348.3 15.9 %all-to-all-start.15 = ((f32[32,24,128]{2,1,0:T(8,128)}), f32[32,24,128]{2,1,0:T(8,128)S(1)}, u32[]{:S(2)}, u32[]{:S(2)}) async-start(f32[32,24,128]{2,1,0:T(8,128)} %get-tuple-element.103), calls=%async_computation.15 | async-start | bytes 786432 | tf_op jit(solution)/shard_map/all_to_all | solution.py:180
Sparse Core Ops, SparseCore 0:
  9.2 38.7 all-gather.8
  49.8 46.2 all-gather.10
  100.3 32.4 all-gather.12
  134.5 34.5 all-gather.14
  170.8 34.5 all-gather.16

commit v3 on v2

--- a/solution.py
+++ b/solution.py
@@ -96,17 +96,17 @@
     copies_ref[...] = jnp.broadcast_to(tile[None], copies_ref.shape)
 
 
-def earlier_kernel(places, follow, *refs):
+def earlier_kernel(places, arrays, follow, *refs):
     count = len(places)
-    base_ref, inverses_ref = refs[:2]
-    panels = refs[2 : 2 + len(follow[1])]
-    parts_refs = refs[2 + len(panels) : 2 + len(panels) + count - 1]
-    base_out, matrix_out, inverse_out, blocks, sems = refs[2 + len(panels) + count - 1 :]
+    base_ref = refs[0]
+    panels = refs[1 : 1 + arrays]
+    parts_refs = refs[1 + arrays : arrays + count]
+    base_out, matrix_out, inverse_out, blocks, sems = refs[arrays + count :]
     targets = [blocks.at[k] for k in range(count - 1)] + [matrix_out]
     copies = []
     for k, (panel, slot) in enumerate(places):
         copies.append(pltpu.make_async_copy(panels[panel].at[slot], targets[k], sems.at[k]))
-    copies.append(pltpu.make_async_copy(inverses_ref.at[follow[0]], inverse_out, sems.at[count]))
+    copies.append(pltpu.make_async_copy(panels[0].at[follow], inverse_out, sems.at[count]))
     for copy in copies:
         copy.start()
     total = base_ref[...]
@@ -134,7 +134,6 @@
     cols = right_side.shape[2] // sections
     half = cols // 2
     f32 = jnp.float32
-    tile = jax.ShapeDtypeStruct((half, LANES), f32)
     tile_in_vmem = pltpu.VMEM((half, LANES), f32)
     copies_in_vmem = pltpu.VMEM((lines, half, LANES), f32)
     parts_in_vmem = pltpu.VMEM((2 * cols, block), jnp.bfloat16)
@@ -152,49 +151,34 @@
     )(right_side[0])
     given = lax.all_to_all(chunks, "sec", 0, 0, tiled=True)
 
-    inverses = lax.all_gather(inverse_blocks[0], "sec", axis=0)
-
-    middle = sections // 2
-
-    def panel(factor, d):
-        far = {1: sections, middle: sections - 1}.get(d, sections - d)
-        own = lax.dynamic_index_in_dim(factor, jnp.minimum(segment + d, sections - 1), 0, False)
-        if far < sections:
-            sent = lax.dynamic_index_in_dim(
-                factor, jnp.minimum(segment + far, sections - 1), 0, False
-            )
-            route = [(k, k + far) for k in range(sections - far)]
-            moved = lax.ppermute(sent, "sec", route)
-            own = jnp.where(segment + d < sections, own, moved)
-        return lax.all_gather(own, "sec", axis=0)
-
-    def place(j, k):
-        d = j - k
-        if d <= middle:
-            return d, k
-        return (middle if d + 1 == sections else sections - d), j
-
-    panels = {1: panel(factor, 1)}
+    def diagonal(d):
+        return lax.dynamic_index_in_dim(factor, jnp.minimum(segment + d, sections - 1), 0, False)
+
+    first = lax.all_gather(jnp.stack([inverse_blocks[0], diagonal(1)]), "sec", axis=0)
+    panels = {1: (first, 1)}
+    for group in ((2,), (3,), (4, 5), (6, 7)):
+        gathered = lax.all_gather(jnp.stack([diagonal(d) for d in group]), "sec", axis=0)
+        panels |= {d: (gathered, line) for line, d in enumerate(group)}
 
     def exchange(copies):
         return lax.all_to_all(copies, "row", 0, 0, tiled=True)
 
     def fetch(i):
         return pl.pallas_call(
-            functools.partial(fetch_kernel, i),
+            functools.partial(fetch_kernel, (i, 0)),
             out_shape=matrix_in_vmem,
             in_specs=[HBM],
             out_specs=VMEM,
             scratch_shapes=[pltpu.SemaphoreType.DMA],
             compiler_params=params,
             name=f"fetch_{i}",
-        )(in_hbm(inverses))
+        )(in_hbm(first))
 
     def apply(i, gathered, inverse):
         last = i + 1 == sections
         return pl.pallas_call(
             last_kernel if last else apply_kernel,
-            out_shape=tile if last else (tile, copies_in_vmem),
+            out_shape=tile_in_vmem if last else (tile_in_vmem, copies_in_vmem),
             in_specs=[VMEM, VMEM],
             out_specs=VMEM if last else (VMEM, VMEM),
             scratch_shapes=[whole_scratch, parts_in_vmem],
@@ -214,13 +198,18 @@
         )(in_vmem(gathered), in_vmem(base), in_vmem(matrix))
 
     def earlier(j, base, known):
-        where = [place(j, k) for k in range(j)]
-        used = sorted({d for d, _ in where})
-        places = [(used.index(d), slot) for d, slot in where]
-        return pl.pallas_call(
-            functools.partial(earlier_kernel, places, (j, used)),
+        arrays = [first]
+        places = []
+        for k in range(j):
+            array, line = panels[j - k]
+            if not any(array is other for other in arrays):
+                arrays.append(array)
+            index = [array is other for other in arrays].index(True)
+            places.append((index, (k, line)))
+        return pl.pallas_call(
+            functools.partial(earlier_kernel, places, len(arrays), (j, 0)),
             out_shape=(tile_in_vmem, matrix_in_vmem, matrix_in_vmem),
-            in_specs=[VMEM, HBM] + [HBM] * len(used) + [VMEM] * len(known),
+            in_specs=[VMEM] + [HBM] * len(arrays) + [VMEM] * len(known),
             out_specs=(VMEM, VMEM, VMEM),
             scratch_shapes=[
                 pltpu.VMEM((max(j - 1, 1), local_rows, block), f32),
@@ -228,12 +217,7 @@
             ],
             compiler_params=params,
             name=f"earlier_{j}",
-        )(
-            base,
-            in_hbm(inverses),
-            *[in_hbm(panels[d]) for d in used],
-            *[in_vmem(parts) for parts in known],
-        )
+        )(base, *[in_hbm(array) for array in arrays], *[in_vmem(parts) for parts in known])
 
     pieces = []
     known = []
@@ -241,9 +225,6 @@
     inverse = fetch(0)
     for i in range(sections):
         gathered = exchange(copies)
-        if i == 0:
-            gathered, factor = lax.optimization_barrier((gathered, factor))
-            panels |= {d: panel(factor, d) for d in range(2, middle + 1)}
         if i + 1 == sections:
             pieces.append(apply(i, gathered, inverse))
             break

time: 389 us -> 356 us (0.915)
  waiting for transfers between devices: 134 us -> 106 us
    ppermute x3 -> x0, waiting for transfers between devices: 41.2 us -> none  [panel(): moved = lax.ppermute(sent, 'sec', route)]
    all_gather x5, waiting for transfers between devices: 0.1 us -> 30.1 us  [the longest x1 30.1 us: shards(): lax.all_gather(jnp.stack([inverse_blocks[0], diagonal(1)]), 'sec', axis=0)]
    all_to_all x9, waiting for transfers between devices: 90.8 us -> 74.5 us  [exchange(): return lax.all_to_all(copies, 'row', 0, 0, tiled=True)]
    ppermute x3 -> x0, starting transfers between devices: 8.09 us -> none  [panel(): moved = lax.ppermute(sent, 'sec', route)]
    all_to_all x9, starting transfers between devices: 52.4 us -> 57.4 us  [exchange(): return lax.all_to_all(copies, 'row', 0, 0, tiled=True)]
    all_to_all x6, blocking collectives: 108 us -> 104 us  [exchange(): return lax.all_to_all(copies, 'row', 0, 0, tiled=True)]
    pallas_call x15 -> x16, Pallas kernels: 28.3 us -> 28.9 us  [the longest x7 18.9 us: earlier(): pl.pallas_call(functools.partial(earlier_kernel, places, len(arrays), (j,...]
  transfers between devices with their start and end apart: 17 -> 14, of which waited for: 11 -> 9; matrix products, arithmetic and copies ran while one was open for 2% -> 2% of each run, Pallas kernels for 7% -> 8%
where the time goes in v3:
time: 356 us; the launch traced here: 355 us
  blocking collectives  132 us (37%)
  waiting for transfers between devices  106 us (30%)
  starting transfers between devices  57.6 us (16%)
  Pallas kernels  33.9 us (10%)
  between operations  13.4 us (4%)
  local copies, waits for them, and re-layouts  8.82 us (2%)
    all_to_all x6, blocking collectives, exchange(): return lax.all_to_all(copies, 'row', 0, 0, tiled=True)  104 us
    all_to_all x9, waiting for transfers between devices, exchange(): return lax.all_to_all(copies, 'row', 0, 0, tiled=True)  74.5 us
    all_to_all x9, starting transfers between devices, exchange(): return lax.all_to_all(copies, 'row', 0, 0, tiled=True)  57.4 us
    all_gather x1, waiting for transfers between devices, shards(): lax.all_gather(jnp.stack([inverse_blocks[0], diagonal(1)]), 'sec', axis=0)  30.1 us
    pallas_call x7, Pallas kernels, earlier(): pl.pallas_call(functools.partial(earlier_kernel, places, len(arrays), (j,...  18.9 us
    all_to_all x1, blocking collectives, shards(): found = lax.all_to_all(jnp.stack(pieces), 'sec', 0, 0, tiled=True)  17.2 us
    all_to_all x1, blocking collectives, shards(): given = lax.all_to_all(chunks, 'sec', 0, 0, tiled=True)  10.8 us
    pallas_call x8, Pallas kernels, apply(): pl.pallas_call(last_kernel if last else apply_kernel, out_shape=tile_in_v...  9 us
  transfers between devices with their start and end apart: 14, of which 9 were waited for; matrix products, arithmetic and copies ran while one was open for 2% of the time, Pallas kernels for 8%

profile of v3, /device:TPU:1, one launch (start us, length us, event | category | flops | bytes accessed | tf_op | source)
XLA Modules:
  0.0 354.6 jit_solution(5665573112473042235)
XLA Ops:
  14.9 10.8 %all_to_all.85 = f32[8,24,128]{2,1,0:T(8,128)S(1)} all-to-all(f32[8,24,128]{2,1,0:T(8,128)S(1)} %pack.1), channel_id=1, replica_groups=mesh['sec'=8,'row'=32] {'sec'}, dimensions={0} | all-to-all | bytes 196608 | tf_op jit(solution)/shard_map/all_to_all | solution.py:152
  26.5 11.2 %all-to-all-start.1 = ((f32[32,24,128]{2,1,0:T(8,128)}), f32[32,24,128]{2,1,0:T(8,128)S(1)}, u32[]{:S(2)}, u32[]{:S(2)}) async-start(f32[32,24,128]{2,1,0:T(8,128)} %broadcast_in_dim.11), calls=%async_computation.1 | async-start | bytes 786432 | tf_op jit(solution)/shard_map/all_to_all | solution.py:164
  37.7 30.1 %all-gather.11.cloned.1.call-done = f32[16,64,2048]{2,1,0:T(8,128)} async-done(((f32[2,64,2048]{2,1,0:T(8,128)}), f32[16,64,2048]{2,1,0:T(8,128)}) %all-gather.11.cloned.1.call-update) | async-done | bytes 8388624 | tf_op jit(solution)/shard_map/all_gather | solution.py:157
  70.1 9.6 %all-to-all-start.2 = ((f32[32,24,128]{2,1,0:T(8,128)}), f32[32,24,128]{2,1,0:T(8,128)S(1)}, u32[]{:S(2)}, u32[]{:S(2)}) async-start(f32[32,24,128]{2,1,0:T(8,128)} %get-tuple-element.54), calls=%async_computation.2 | async-start | bytes 786432 | tf_op jit(solution)/shard_map/all_to_all | solution.py:164
  80.9 12.8 %all-to-all-done.2.gathered_ref = f32[32,24,128]{2,1,0:T(8,128)S(1)} async-done(((f32[32,24,128]{2,1,0:T(8,128)}), f32[32,24,128]{2,1,0:T(8,128)S(1)}, u32[]{:S(2)}, u32[]{:S(2)}) %all-to-all-start.2) | async-done | bytes 393248 | tf_op jit(solution)/shard_map/all_to_all | solution.py:164
  94.2 17.4 %all_to_all.86.gathered_ref = f32[32,24,128]{2,1,0:T(8,128)S(1)} all-to-all(f32[32,24,128]{2,1,0:T(8,128)S(1)} %get-tuple-element.57), channel_id=1, replica_groups=mesh['sec'=8,'row'=32] {'row'}, dimensions={0} | all-to-all | bytes 786432 | tf_op jit(solution)/shard_map/all_to_all | solution.py:164
  112.8 5.8 %all-to-all-start.4 = ((f32[32,24,128]{2,1,0:T(8,128)}), f32[32,24,128]{2,1,0:T(8,128)S(1)}, u32[]{:S(2)}, u32[]{:S(2)}) async-start(f32[32,24,128]{2,1,0:T(8,128)} %get-tuple-element.60), calls=%async_computation.4 | async-start | bytes 786432 | tf_op jit(solution)/shard_map/all_to_all | solution.py:164
  120.3 11.2 %all-to-all-done.4.gathered_ref = f32[32,24,128]{2,1,0:T(8,128)S(1)} async-done(((f32[32,24,128]{2,1,0:T(8,128)}), f32[32,24,128]{2,1,0:T(8,128)S(1)}, u32[]{:S(2)}, u32[]{:S(2)}) %all-to-all-start.4) | async-done | bytes 393248 | tf_op jit(solution)/shard_map/all_to_all | solution.py:164
  132.0 18.0 %all_to_all.87.gathered_ref = f32[32,24,128]{2,1,0:T(8,128)S(1)} all-to-all(f32[32,24,128]{2,1,0:T(8,128)S(1)} %get-tuple-element.64), channel_id=1, replica_groups=mesh['sec'=8,'row'=32] {'row'}, dimensions={0} | all-to-all | bytes 786432 | tf_op jit(solution)/shard_map/all_to_all | solution.py:164
  151.2 5.8 %all-to-all-start.6 = ((f32[32,24,128]{2,1,0:T(8,128)}), f32[32,24,128]{2,1,0:T(8,128)S(1)}, u32[]{:S(2)}, u32[]{:S(2)}) async-start(f32[32,24,128]{2,1,0:T(8,128)} %get-tuple-element.67), calls=%async_computation.6 | async-start | bytes 786432 | tf_op jit(solution)/shard_map/all_to_all | solution.py:164
  159.2 10.3 %all-to-all-done.6.gathered_ref = f32[32,24,128]{2,1,0:T(8,128)S(1)} async-done(((f32[32,24,128]{2,1,0:T(8,128)}), f32[32,24,128]{2,1,0:T(8,128)S(1)}, u32[]{:S(2)}, u32[]{:S(2)}) %all-to-all-start.6) | async-done | bytes 393248 | tf_op jit(solution)/shard_map/all_to_all | solution.py:164
  170.0 18.2 %all_to_all.88.gathered_ref = f32[32,24,128]{2,1,0:T(8,128)S(1)} all-to-all(f32[32,24,128]{2,1,0:T(8,128)S(1)} %get-tuple-element.71), channel_id=1, replica_groups=mesh['sec'=8,'row'=32] {'row'}, dimensions={0} | all-to-all | bytes 786432 | tf_op jit(solution)/shard_map/all_to_all | solution.py:164
  189.4 5.7 %all-to-all-start.8 = ((f32[32,24,128]{2,1,0:T(8,128)}), f32[32,24,128]{2,1,0:T(8,128)S(1)}, u32[]{:S(2)}, u32[]{:S(2)}) async-start(f32[32,24,128]{2,1,0:T(8,128)} %get-tuple-element.74), calls=%async_computation.8 | async-start | bytes 786432 | tf_op jit(solution)/shard_map/all_to_all | solution.py:164
  197.7 9.3 %all-to-all-done.8.gathered_ref = f32[32,24,128]{2,1,0:T(8,128)S(1)} async-done(((f32[32,24,128]{2,1,0:T(8,128)}), f32[32,24,128]{2,1,0:T(8,128)S(1)}, u32[]{:S(2)}, u32[]{:S(2)}) %all-to-all-start.8) | async-done | bytes 393248 | tf_op jit(solution)/shard_map/all_to_all | solution.py:164
  207.4 17.9 %all_to_all.89.gathered_ref = f32[32,24,128]{2,1,0:T(8,128)S(1)} all-to-all(f32[32,24,128]{2,1,0:T(8,128)S(1)} %get-tuple-element.78), channel_id=1, replica_groups=mesh['sec'=8,'row'=32] {'row'}, dimensions={0} | all-to-all | bytes 786432 | tf_op jit(solution)/shard_map/all_to_all | solution.py:164
  226.6 5.9 %all-to-all-start.10 = ((f32[32,24,128]{2,1,0:T(8,128)}), f32[32,24,128]{2,1,0:T(8,128)S(1)}, u32[]{:S(2)}, u32[]{:S(2)}) async-start(f32[32,24,128]{2,1,0:T(8,128)} %get-tuple-element.81), calls=%async_computation.10 | async-start | bytes 786432 | tf_op jit(solution)/shard_map/all_to_all | solution.py:164
  235.8 8.4 %all-to-all-done.10.gathered_ref = f32[32,24,128]{2,1,0:T(8,128)S(1)} async-done(((f32[32,24,128]{2,1,0:T(8,128)}), f32[32,24,128]{2,1,0:T(8,128)S(1)}, u32[]{:S(2)}, u32[]{:S(2)}) %all-to-all-start.10) | async-done | bytes 393248 | tf_op jit(solution)/shard_map/all_to_all | solution.py:164
  244.7 16.9 %all_to_all.90.gathered_ref = f32[32,24,128]{2,1,0:T(8,128)S(1)} all-to-all(f32[32,24,128]{2,1,0:T(8,128)S(1)} %get-tuple-element.85), channel_id=1, replica_groups=mesh['sec'=8,'row'=32] {'row'}, dimensions={0} | all-to-all | bytes 786432 | tf_op jit(solution)/shard_map/all_to_all | solution.py:164
  262.9 5.6 %all-to-all-start.12 = ((f32[32,24,128]{2,1,0:T(8,128)}), f32[32,24,128]{2,1,0:T(8,128)S(1)}, u32[]{:S(2)}, u32[]{:S(2)}) async-start(f32[32,24,128]{2,1,0:T(8,128)} %get-tuple-element.88), calls=%async_computation.12 | async-start | bytes 786432 | tf_op jit(solution)/shard_map/all_to_all | solution.py:164
  272.2 7.9 %all-to-all-done.12.gathered_ref = f32[32,24,128]{2,1,0:T(8,128)S(1)} async-done(((f32[32,24,128]{2,1,0:T(8,128)}), f32[32,24,128]{2,1,0:T(8,128)S(1)}, u32[]{:S(2)}, u32[]{:S(2)}) %all-to-all-start.12) | async-done | bytes 393248 | tf_op jit(solution)/shard_map/all_to_all | solution.py:164
  280.5 15.2 %all_to_all.91.gathered_ref = f32[32,24,128]{2,1,0:T(8,128)S(1)} all-to-all(f32[32,24,128]{2,1,0:T(8,128)S(1)} %get-tuple-element.92), channel_id=1, replica_groups=mesh['sec'=8,'row'=32] {'row'}, dimensions={0} | all-to-all | bytes 786432 | tf_op jit(solution)/shard_map/all_to_all | solution.py:164
  307.0 5.5 %all-to-all-done.14.gathered_ref = f32[32,24,128]{2,1,0:T(8,128)S(1)} async-done(((f32[32,24,128]{2,1,0:T(8,128)}), f32[32,24,128]{2,1,0:T(8,128)S(1)}, u32[]{:S(2)}, u32[]{:S(2)}) %all-to-all-start.14) | async-done | bytes 393248 | tf_op jit(solution)/shard_map/all_to_all | solution.py:164
  320.0 9.0 %all-to-all-done.15.gathered_ref = f32[32,24,128]{2,1,0:T(8,128)S(1)} async-done(((f32[32,24,128]{2,1,0:T(8,128)}), f32[32,24,128]{2,1,0:T(8,128)S(1)}, u32[]{:S(2)}, u32[]{:S(2)}) %all-to-all-start.15) | async-done | bytes 393248 | tf_op jit(solution)/shard_map/all_to_all | solution.py:164
  330.1 17.2 %all_to_all.92.packed_ref = f32[8,24,128]{2,1,0:T(8,128)S(1)} all-to-all(f32[8,24,128]{2,1,0:T(8,128)} %constant_dynamic-update-slice_fusion), channel_id=1, replica_groups=mesh['sec'=8,'row'=32] {'sec'}, dimensions={0} | all-to-all | bytes 196608 | tf_op jit(solution)/shard_map/all_to_all | solution.py:238
  (66 shorter events, 55.5 us)
Async XLA Ops:
  6.5 3.3 copy-start.3
  6.5 61.2 %all-gather.11.cloned.1.call-start = ((), (), s32[]{:S(2)}) async-start(), calls=%async_computation.17 | async-start | bytes 9437184 | tf_op jit(solution)/shard_map/all_gather | solution.py:157
  11.0 3.8 %copy-start.2 = (f32[1,64,384]{2,1,0:T(8,128)S(1)}, f32[1,64,384]{2,1,0:T(8,128)}, u32[]{:S(2)}) copy-start(f32[1,64,384]{2,1,0:T(8,128)} %param.5) | copy-start | bytes 294916
  11.0 107.6 %all-gather.13.cloned.1.call-start = ((), (), s32[]{:S(2)}) async-start(), calls=%async_computation.18 | async-start | bytes 4718592 | tf_op jit(solution)/shard_map/all_gather | solution.py:160
  11.8 145.2 %all-gather.15.cloned.1.call-start = ((), (), s32[]{:S(2)}) async-start(), calls=%async_computation.19 | async-start | bytes 4718592 | tf_op jit(solution)/shard_map/all_gather | solution.py:160
  12.5 182.6 %all-gather.17.cloned.1.call-start = ((), (), s32[]{:S(2)}) async-start(), calls=%async_computation.20 | async-start | bytes 9437184 | tf_op jit(solution)/shard_map/all_gather | solution.py:160
  13.6 254.9 %all-gather.19.cloned.1.call-start = ((), (), s32[]{:S(2)}) async-start(), calls=%async_computation.21 | async-start | bytes 9437184 | tf_op jit(solution)/shard_map/all_gather | solution.py:160
  26.5 42.3 %all-to-all-start.1 = ((f32[32,24,128]{2,1,0:T(8,128)}), f32[32,24,128]{2,1,0:T(8,128)S(1)}, u32[]{:S(2)}, u32[]{:S(2)}) async-start(f32[32,24,128]{2,1,0:T(8,128)} %broadcast_in_dim.11), calls=%async_computation.1 | async-start | bytes 786432 | tf_op jit(solution)/shard_map/all_to_all | solution.py:164
  70.1 23.7 %all-to-all-start.2 = ((f32[32,24,128]{2,1,0:T(8,128)}), f32[32,24,128]{2,1,0:T(8,128)S(1)}, u32[]{:S(2)}, u32[]{:S(2)}) async-start(f32[32,24,128]{2,1,0:T(8,128)} %get-tuple-element.54), calls=%async_computation.2 | async-start | bytes 786432 | tf_op jit(solution)/shard_map/all_to_all | solution.py:164
  112.8 18.7 %all-to-all-start.4 = ((f32[32,24,128]{2,1,0:T(8,128)}), f32[32,24,128]{2,1,0:T(8,128)S(1)}, u32[]{:S(2)}, u32[]{:S(2)}) async-start(f32[32,24,128]{2,1,0:T(8,128)} %get-tuple-element.60), calls=%async_computation.4 | async-start | bytes 786432 | tf_op jit(solution)/shard_map/all_to_all | solution.py:164
  151.2 18.4 %all-to-all-start.6 = ((f32[32,24,128]{2,1,0:T(8,128)}), f32[32,24,128]{2,1,0:T(8,128)S(1)}, u32[]{:S(2)}, u32[]{:S(2)}) async-start(f32[32,24,128]{2,1,0:T(8,128)} %get-tuple-element.67), calls=%async_computation.6 | async-start | bytes 786432 | tf_op jit(solution)/shard_map/all_to_all | solution.py:164
  189.4 17.6 %all-to-all-start.8 = ((f32[32,24,128]{2,1,0:T(8,128)}), f32[32,24,128]{2,1,0:T(8,128)S(1)}, u32[]{:S(2)}, u32[]{:S(2)}) async-start(f32[32,24,128]{2,1,0:T(8,128)} %get-tuple-element.74), calls=%async_computation.8 | async-start | bytes 786432 | tf_op jit(solution)/shard_map/all_to_all | solution.py:164
  226.6 17.6 %all-to-all-start.10 = ((f32[32,24,128]{2,1,0:T(8,128)}), f32[32,24,128]{2,1,0:T(8,128)S(1)}, u32[]{:S(2)}, u32[]{:S(2)}) async-start(f32[32,24,128]{2,1,0:T(8,128)} %get-tuple-element.81), calls=%async_computation.10 | async-start | bytes 786432 | tf_op jit(solution)/shard_map/all_to_all | solution.py:164
  262.9 17.2 %all-to-all-start.12 = ((f32[32,24,128]{2,1,0:T(8,128)}), f32[32,24,128]{2,1,0:T(8,128)S(1)}, u32[]{:S(2)}, u32[]{:S(2)}) async-start(f32[32,24,128]{2,1,0:T(8,128)} %get-tuple-element.88), calls=%async_computation.12 | async-start | bytes 786432 | tf_op jit(solution)/shard_map/all_to_all | solution.py:164
  280.5 16.5 %copy-start = (bf16[96,2048]{1,0:T(8,128)(2,1)}, bf16[96,2048]{1,0:T(8,128)(2,1)S(1)}, u32[]{:S(2)}) copy-start(bf16[96,2048]{1,0:T(8,128)(2,1)S(1)} %get-tuple-element.96.refs_11_) | copy-start | bytes 1179652
  297.0 15.4 %all-to-all-start.14 = ((f32[32,24,128]{2,1,0:T(8,128)}), f32[32,24,128]{2,1,0:T(8,128)S(1)}, u32[]{:S(2)}, u32[]{:S(2)}) async-start(f32[32,24,128]{2,1,0:T(8,128)} %get-tuple-element.95), calls=%async_computation.14 | async-start | bytes 786432 | tf_op jit(solution)/shard_map/all_to_all | solution.py:164
  301.0 0.6 copy-start.4
  301.6 1.0 copy-start.1
  313.6 15.4 %all-to-all-start.15 = ((f32[32,24,128]{2,1,0:T(8,128)}), f32[32,24,128]{2,1,0:T(8,128)S(1)}, u32[]{:S(2)}, u32[]{:S(2)}) async-start(f32[32,24,128]{2,1,0:T(8,128)} %get-tuple-element.99), calls=%async_computation.15 | async-start | bytes 786432 | tf_op jit(solution)/shard_map/all_to_all | solution.py:164
Sparse Core Ops, SparseCore 0:
  11.1 56.5 all-gather.10
  69.6 34.7 all-gather.12
  106.3 34.5 all-gather.14
  142.6 52.1 all-gather.16
  196.6 52.3 all-gather.18

commit v4 on v3

--- a/solution.py
+++ b/solution.py
@@ -85,9 +85,13 @@
     copies_ref[...] = jnp.broadcast_to(tile[None], copies_ref.shape)
 
 
-def last_kernel(gathered_ref, matrix_ref, tile_ref, whole, parts):
+def last_kernel(gathered_ref, matrix_ref, *refs):
+    earlier_refs = refs[:-3]
+    out_ref, whole, parts = refs[-3:]
+    for i, piece_ref in enumerate(earlier_refs):
+        out_ref[i] = piece_ref[...]
     spread(gathered_ref, whole, parts)
-    tile_ref[...] = packed(times(parts[...], matrix_ref[...]))
+    out_ref[len(earlier_refs)] = packed(times(parts[...], matrix_ref[...]))
 
 
 def residual_kernel(gathered_ref, base_ref, matrix_ref, copies_ref, parts, whole):
@@ -151,40 +155,50 @@
     )(right_side[0])
     given = lax.all_to_all(chunks, "sec", 0, 0, tiled=True)
 
-    def diagonal(d):
-        return lax.dynamic_index_in_dim(factor, jnp.minimum(segment + d, sections - 1), 0, False)
-
-    first = lax.all_gather(jnp.stack([inverse_blocks[0], diagonal(1)]), "sec", axis=0)
-    panels = {1: (first, 1)}
-    for group in ((2,), (3,), (4, 5), (6, 7)):
-        gathered = lax.all_gather(jnp.stack([diagonal(d) for d in group]), "sec", axis=0)
-        panels |= {d: (gathered, line) for line, d in enumerate(group)}
+    def panel(factor, d):
+        own = lax.dynamic_index_in_dim(factor, jnp.minimum(segment + d, sections - 1), 0, False)
+        return lax.all_gather(own, "sec", axis=0)
+
+    inverses = lax.all_gather(inverse_blocks[0], "sec", axis=0)
+    panels = {1: panel(factor, 1)}
+    given, factor = lax.optimization_barrier((given, factor))
+    panels |= {d: panel(factor, d) for d in range(2, sections)}
 
     def exchange(copies):
         return lax.all_to_all(copies, "row", 0, 0, tiled=True)
 
     def fetch(i):
         return pl.pallas_call(
-            functools.partial(fetch_kernel, (i, 0)),
+            functools.partial(fetch_kernel, i),
             out_shape=matrix_in_vmem,
             in_specs=[HBM],
             out_specs=VMEM,
             scratch_shapes=[pltpu.SemaphoreType.DMA],
             compiler_params=params,
             name=f"fetch_{i}",
-        )(in_hbm(first))
+        )(in_hbm(inverses))
 
     def apply(i, gathered, inverse):
-        last = i + 1 == sections
-        return pl.pallas_call(
-            last_kernel if last else apply_kernel,
-            out_shape=tile_in_vmem if last else (tile_in_vmem, copies_in_vmem),
+        return pl.pallas_call(
+            apply_kernel,
+            out_shape=(tile_in_vmem, copies_in_vmem),
             in_specs=[VMEM, VMEM],
-            out_specs=VMEM if last else (VMEM, VMEM),
+            out_specs=(VMEM, VMEM),
             scratch_shapes=[whole_scratch, parts_in_vmem],
             compiler_params=params,
             name=f"apply_{i}",
         )(in_vmem(gathered), in_vmem(inverse))
+
+    def apply_last(gathered, inverse, pieces):
+        return pl.pallas_call(
+            last_kernel,
+            out_shape=pltpu.VMEM((sections, half, LANES), f32),
+            in_specs=[VMEM, VMEM] + [VMEM] * len(pieces),
+            out_specs=VMEM,
+            scratch_shapes=[whole_scratch, parts_in_vmem],
+            compiler_params=params,
+            name="apply_last",
+        )(in_vmem(gathered), in_vmem(inverse), *[in_vmem(piece) for piece in pieces])
 
     def residual(j, gathered, base, matrix):
         return pl.pallas_call(
@@ -198,16 +212,10 @@
         )(in_vmem(gathered), in_vmem(base), in_vmem(matrix))
 
     def earlier(j, base, known):
-        arrays = [first]
-        places = []
-        for k in range(j):
-            array, line = panels[j - k]
-            if not any(array is other for other in arrays):
-                arrays.append(array)
-            index = [array is other for other in arrays].index(True)
-            places.append((index, (k, line)))
-        return pl.pallas_call(
-            functools.partial(earlier_kernel, places, len(arrays), (j, 0)),
+        arrays = [inverses, *(panels[j - k] for k in range(j))]
+        places = [(1 + k, k) for k in range(j)]
+        return pl.pallas_call(
+            functools.partial(earlier_kernel, places, len(arrays), j),
             out_shape=(tile_in_vmem, matrix_in_vmem, matrix_in_vmem),
             in_specs=[VMEM] + [HBM] * len(arrays) + [VMEM] * len(known),
             out_specs=(VMEM, VMEM, VMEM),
@@ -226,7 +234,7 @@
     for i in range(sections):
         gathered = exchange(copies)
         if i + 1 == sections:
-            pieces.append(apply(i, gathered, inverse))
+            stacked = apply_last(gathered, inverse, pieces)
             break
         piece, copies = apply(i, gathered, inverse)
         pieces.append(piece)
@@ -235,7 +243,7 @@
         copies, parts = residual(i + 1, gathered, base, matrix)
         known.append(parts)
 
-    found = lax.all_to_all(jnp.stack(pieces), "sec", 0, 0, tiled=True)
+    found = lax.all_to_all(stacked, "sec", 0, 0, tiled=True)
     out = pl.pallas_call(
         unpack_kernel,
         out_shape=jax.ShapeDtypeStruct(right_side.shape[1:], f32),

time: 356 us -> 355 us (level)
  blocking collectives: 132 us -> 123 us
  waiting for transfers between devices: 106 us -> 113 us
    all_to_all x2 -> x1, blocking collectives: 28 us -> 14.5 us  [shards(): found = lax.all_to_all(stacked, 'sec', 0, 0, tiled=True)]
    all_to_all x9, waiting for transfers between devices: 74.5 us -> 63.6 us  [exchange(): return lax.all_to_all(copies, 'row', 0, 0, tiled=True)]
    all_gather x5 -> x8, waiting for transfers between devices: 30.1 us -> 40.3 us  [the longest x7 32.2 us: panel(): return lax.all_gather(own, 'sec', axis=0)]
    all_to_all x0 -> x1, starting transfers between devices: none -> 6.46 us  [shards(): given = lax.all_to_all(chunks, 'sec', 0, 0, tiled=True)]
    all_to_all x0 -> x1, waiting for transfers between devices: none -> 5 us  [shards(): given = lax.all_to_all(chunks, 'sec', 0, 0, tiled=True)]
    all_to_all x6, blocking collectives: 104 us -> 109 us  [exchange(): return lax.all_to_all(copies, 'row', 0, 0, tiled=True)]
  transfers between devices with their start and end apart: 14 -> 18, of which waited for: 9 -> 15; matrix products, arithmetic and copies ran while one was open for 2% -> 2% of each run, Pallas kernels for 8% -> 9%
where the time goes in v4:
time: 355 us; the launch traced here: 353 us
  blocking collectives  123 us (35%)
  waiting for transfers between devices  113 us (32%)
  starting transfers between devices  60.8 us (17%)
  Pallas kernels  34.8 us (10%)
  between operations  13.7 us (4%)
  local copies, waits for them, and re-layouts  8.07 us (2%)
    all_to_all x6, blocking collectives, exchange(): return lax.all_to_all(copies, 'row', 0, 0, tiled=True)  109 us
    all_to_all x9, waiting for transfers between devices, exchange(): return lax.all_to_all(copies, 'row', 0, 0, tiled=True)  63.6 us
    all_to_all x9, starting transfers between devices, exchange(): return lax.all_to_all(copies, 'row', 0, 0, tiled=True)  54.1 us
    all_gather x7, waiting for transfers between devices, panel(): return lax.all_gather(own, 'sec', axis=0)  32.2 us
    pallas_call x7, Pallas kernels, earlier(): pl.pallas_call(functools.partial(earlier_kernel, places, len(arrays), j),...  18.6 us
    all_to_all x1, blocking collectives, shards(): found = lax.all_to_all(stacked, 'sec', 0, 0, tiled=True)  14.5 us
    pallas_call x7, Pallas kernels, apply(): pl.pallas_call(apply_kernel, out_shape=(tile_in_vmem, copies_in_vmem), in...  8.54 us
    all_gather x1, waiting for transfers between devices, shards(): inverses = lax.all_gather(inverse_blocks[0], 'sec', axis=0)  8.17 us
  transfers between devices with their start and end apart: 18, of which 15 were waited for; matrix products, arithmetic and copies ran while one was open for 2% of the time, Pallas kernels for 9%

profile of v4, /device:TPU:1, one launch (start us, length us, event | category | flops | bytes accessed | tf_op | source)
XLA Modules:
  0.0 353.1 jit_solution(8915108755330162162)
XLA Ops:
  10.9 6.5 %all-to-all-start = ((f32[8,24,128]{2,1,0:T(8,128)}), f32[8,24,128]{2,1,0:T(8,128)S(1)}, u32[]{:S(2)}, u32[]{:S(2)}) async-start(f32[8,24,128]{2,1,0:T(8,128)} %pack.1), calls=%async_computation | async-start | bytes 196608 | tf_op jit(solution)/shard_map/all_to_all | solution.py:156
  29.2 10.6 %all-to-all-start.1 = ((f32[32,24,128]{2,1,0:T(8,128)}), f32[32,24,128]{2,1,0:T(8,128)S(1)}, u32[]{:S(2)}, u32[]{:S(2)}) async-start(f32[32,24,128]{2,1,0:T(8,128)} %broadcast_in_dim.11), calls=%async_computation.1 | async-start | bytes 786432 | tf_op jit(solution)/shard_map/all_to_all | solution.py:168
  39.8 8.2 %all-gather.9.cloned.1.call-done.matrix_ref.refs_1_ = f32[8,64,2048]{2,1,0:T(8,128)} async-done(((f32[1,64,2048]{2,1,0:T(8,128)}), f32[8,64,2048]{2,1,0:T(8,128)}) %all-gather.9.cloned.1.call-update) | async-done | bytes 4194320 | tf_op jit(solution)/shard_map/all_gather | solution.py:162
  59.9 24.5 %all-gather.11.cloned.1.call-done.refs_2_.refs_3_.refs_4_.refs_5_.refs_6_.refs_7_.refs_8_ = f32[8,64,2048]{2,1,0:T(8,128)} async-done(((f32[1,64,2048]{2,1,0:T(8,128)}), f32[8,64,2048]{2,1,0:T(8,128)}) %all-gather.11.cloned.1.call-update) | async-done | bytes 4194320 | tf_op jit(solution)/shard_map/all_gather | solution.py:160
  86.2 23.5 %all_to_all.85.gathered_ref = f32[32,24,128]{2,1,0:T(8,128)S(1)} all-to-all(f32[32,24,128]{2,1,0:T(8,128)S(1)} %get-tuple-element.59), channel_id=1, replica_groups=mesh['sec'=8,'row'=32] {'row'}, dimensions={0} | all-to-all | bytes 786432 | tf_op jit(solution)/shard_map/all_to_all | solution.py:168
  115.6 5.3 %all-gather.13.cloned.1.call-done.refs_2_.refs_3_.refs_4_.refs_5_.refs_6_.refs_7_ = f32[8,64,2048]{2,1,0:T(8,128)} async-done(((f32[1,64,2048]{2,1,0:T(8,128)}), f32[8,64,2048]{2,1,0:T(8,128)}) %all-gather.13.cloned.1.call-update) | async-done | bytes 4194320 | tf_op jit(solution)/shard_map/all_gather | solution.py:160
  122.4 6.1 %all-to-all-done.4.gathered_ref = f32[32,24,128]{2,1,0:T(8,128)S(1)} async-done(((f32[32,24,128]{2,1,0:T(8,128)}), f32[32,24,128]{2,1,0:T(8,128)S(1)}, u32[]{:S(2)}, u32[]{:S(2)}) %all-to-all-start.4) | async-done | bytes 393248 | tf_op jit(solution)/shard_map/all_to_all | solution.py:168
  129.7 5.8 %all-to-all-start.5 = ((f32[32,24,128]{2,1,0:T(8,128)}), f32[32,24,128]{2,1,0:T(8,128)S(1)}, u32[]{:S(2)}, u32[]{:S(2)}) async-start(f32[32,24,128]{2,1,0:T(8,128)} %get-tuple-element.66), calls=%async_computation.5 | async-start | bytes 786432 | tf_op jit(solution)/shard_map/all_to_all | solution.py:168
  136.2 12.1 %all-to-all-done.5.gathered_ref = f32[32,24,128]{2,1,0:T(8,128)S(1)} async-done(((f32[32,24,128]{2,1,0:T(8,128)}), f32[32,24,128]{2,1,0:T(8,128)S(1)}, u32[]{:S(2)}, u32[]{:S(2)}) %all-to-all-start.5) | async-done | bytes 393248 | tf_op jit(solution)/shard_map/all_to_all | solution.py:168
  149.6 5.6 %all-to-all-start.6 = ((f32[32,24,128]{2,1,0:T(8,128)}), f32[32,24,128]{2,1,0:T(8,128)S(1)}, u32[]{:S(2)}, u32[]{:S(2)}) async-start(f32[32,24,128]{2,1,0:T(8,128)} %get-tuple-element.68), calls=%async_computation.6 | async-start | bytes 786432 | tf_op jit(solution)/shard_map/all_to_all | solution.py:168
  159.4 8.4 %all-to-all-done.6.gathered_ref = f32[32,24,128]{2,1,0:T(8,128)S(1)} async-done(((f32[32,24,128]{2,1,0:T(8,128)}), f32[32,24,128]{2,1,0:T(8,128)S(1)}, u32[]{:S(2)}, u32[]{:S(2)}) %all-to-all-start.6) | async-done | bytes 393248 | tf_op jit(solution)/shard_map/all_to_all | solution.py:168
  168.2 18.2 %all_to_all.86.gathered_ref = f32[32,24,128]{2,1,0:T(8,128)S(1)} all-to-all(f32[32,24,128]{2,1,0:T(8,128)S(1)} %get-tuple-element.72), channel_id=1, replica_groups=mesh['sec'=8,'row'=32] {'row'}, dimensions={0} | all-to-all | bytes 786432 | tf_op jit(solution)/shard_map/all_to_all | solution.py:168
  187.6 5.8 %all-to-all-start.8 = ((f32[32,24,128]{2,1,0:T(8,128)}), f32[32,24,128]{2,1,0:T(8,128)S(1)}, u32[]{:S(2)}, u32[]{:S(2)}) async-start(f32[32,24,128]{2,1,0:T(8,128)} %get-tuple-element.74), calls=%async_computation.8 | async-start | bytes 786432 | tf_op jit(solution)/shard_map/all_to_all | solution.py:168
  196.1 9.9 %all-to-all-done.8.gathered_ref = f32[32,24,128]{2,1,0:T(8,128)S(1)} async-done(((f32[32,24,128]{2,1,0:T(8,128)}), f32[32,24,128]{2,1,0:T(8,128)S(1)}, u32[]{:S(2)}, u32[]{:S(2)}) %all-to-all-start.8) | async-done | bytes 393248 | tf_op jit(solution)/shard_map/all_to_all | solution.py:168
  206.5 17.3 %all_to_all.87.gathered_ref = f32[32,24,128]{2,1,0:T(8,128)S(1)} all-to-all(f32[32,24,128]{2,1,0:T(8,128)S(1)} %get-tuple-element.78), channel_id=1, replica_groups=mesh['sec'=8,'row'=32] {'row'}, dimensions={0} | all-to-all | bytes 786432 | tf_op jit(solution)/shard_map/all_to_all | solution.py:168
  225.0 6.2 %all-to-all-start.10 = ((f32[32,24,128]{2,1,0:T(8,128)}), f32[32,24,128]{2,1,0:T(8,128)S(1)}, u32[]{:S(2)}, u32[]{:S(2)}) async-start(f32[32,24,128]{2,1,0:T(8,128)} %get-tuple-element.80), calls=%async_computation.10 | async-start | bytes 786432 | tf_op jit(solution)/shard_map/all_to_all | solution.py:168
  234.5 8.7 %all-to-all-done.10.gathered_ref = f32[32,24,128]{2,1,0:T(8,128)S(1)} async-done(((f32[32,24,128]{2,1,0:T(8,128)}), f32[32,24,128]{2,1,0:T(8,128)S(1)}, u32[]{:S(2)}, u32[]{:S(2)}) %all-to-all-start.10) | async-done | bytes 393248 | tf_op jit(solution)/shard_map/all_to_all | solution.py:168
  243.7 17.4 %all_to_all.88.gathered_ref = f32[32,24,128]{2,1,0:T(8,128)S(1)} all-to-all(f32[32,24,128]{2,1,0:T(8,128)S(1)} %get-tuple-element.84), channel_id=1, replica_groups=mesh['sec'=8,'row'=32] {'row'}, dimensions={0} | all-to-all | bytes 786432 | tf_op jit(solution)/shard_map/all_to_all | solution.py:168
  262.3 5.7 %all-to-all-start.12 = ((f32[32,24,128]{2,1,0:T(8,128)}), f32[32,24,128]{2,1,0:T(8,128)S(1)}, u32[]{:S(2)}, u32[]{:S(2)}) async-start(f32[32,24,128]{2,1,0:T(8,128)} %get-tuple-element.86), calls=%async_computation.12 | async-start | bytes 786432 | tf_op jit(solution)/shard_map/all_to_all | solution.py:168
  271.7 7.8 %all-to-all-done.12.gathered_ref = f32[32,24,128]{2,1,0:T(8,128)S(1)} async-done(((f32[32,24,128]{2,1,0:T(8,128)}), f32[32,24,128]{2,1,0:T(8,128)S(1)}, u32[]{:S(2)}, u32[]{:S(2)}) %all-to-all-start.12) | async-done | bytes 393248 | tf_op jit(solution)/shard_map/all_to_all | solution.py:168
  279.9 16.9 %all_to_all.89.gathered_ref = f32[32,24,128]{2,1,0:T(8,128)S(1)} all-to-all(f32[32,24,128]{2,1,0:T(8,128)S(1)} %get-tuple-element.90), channel_id=1, replica_groups=mesh['sec'=8,'row'=32] {'row'}, dimensions={0} | all-to-all | bytes 786432 | tf_op jit(solution)/shard_map/all_to_all | solution.py:168
  308.1 6.1 %all-to-all-done.14.gathered_ref = f32[32,24,128]{2,1,0:T(8,128)S(1)} async-done(((f32[32,24,128]{2,1,0:T(8,128)}), f32[32,24,128]{2,1,0:T(8,128)S(1)}, u32[]{:S(2)}, u32[]{:S(2)}) %all-to-all-start.14) | async-done | bytes 393248 | tf_op jit(solution)/shard_map/all_to_all | solution.py:168
  315.2 15.4 %all_to_all.90.gathered_ref = f32[32,24,128]{2,1,0:T(8,128)S(1)} all-to-all(f32[32,24,128]{2,1,0:T(8,128)S(1)} %get-tuple-element.96), channel_id=1, replica_groups=mesh['sec'=8,'row'=32] {'row'}, dimensions={0} | all-to-all | bytes 786432 | tf_op jit(solution)/shard_map/all_to_all | solution.py:168
  331.0 14.5 %all_to_all.91.packed_ref = f32[8,24,128]{2,1,0:T(8,128)S(1)} all-to-all(f32[8,24,128]{2,1,0:T(8,128)S(1)} %apply_last.1), channel_id=1, replica_groups=mesh['sec'=8,'row'=32] {'sec'}, dimensions={0} | all-to-all | bytes 196608 | tf_op jit(solution)/shard_map/all_to_all | solution.py:246
  (62 shorter events, 73.2 us)
Async XLA Ops:
  6.5 41.5 %all-gather.9.cloned.1.call-start = ((), (), s32[]{:S(2)}) async-start(), calls=%async_computation.17 | async-start | bytes 4718592 | tf_op jit(solution)/shard_map/all_gather | solution.py:162
  7.3 77.2 %all-gather.11.cloned.1.call-start = ((), (), s32[]{:S(2)}) async-start(), calls=%async_computation.18 | async-start | bytes 4718592 | tf_op jit(solution)/shard_map/all_gather | solution.py:160
  9.2 0.9 copy-start.2
  10.9 11.5 %all-to-all-start = ((f32[8,24,128]{2,1,0:T(8,128)}), f32[8,24,128]{2,1,0:T(8,128)S(1)}, u32[]{:S(2)}, u32[]{:S(2)}) async-start(f32[8,24,128]{2,1,0:T(8,128)} %pack.1), calls=%async_computation | async-start | bytes 196608 | tf_op jit(solution)/shard_map/all_to_all | solution.py:156
  17.3 103.6 %all-gather.13.cloned.1.call-start = ((), (), s32[]{:S(2)}) async-start(), calls=%async_computation.19 | async-start | bytes 4718592 | tf_op jit(solution)/shard_map/all_gather | solution.py:160
  25.9 131.4 %all-gather.15.cloned.1.call-start = ((), (), s32[]{:S(2)}) async-start(), calls=%async_computation.20 | async-start | bytes 4718592 | tf_op jit(solution)/shard_map/all_gather | solution.py:160
  26.5 167.1 %all-gather.17.cloned.1.call-start = ((), (), s32[]{:S(2)}) async-start(), calls=%async_computation.21 | async-start | bytes 4718592 | tf_op jit(solution)/shard_map/all_gather | solution.py:160
  27.0 204.2 %all-gather.19.cloned.1.call-start = ((), (), s32[]{:S(2)}) async-start(), calls=%async_computation.22 | async-start | bytes 4718592 | tf_op jit(solution)/shard_map/all_gather | solution.py:160
  27.6 240.4 %all-gather.21.cloned.1.call-start = ((), (), s32[]{:S(2)}) async-start(), calls=%async_computation.23 | async-start | bytes 4718592 | tf_op jit(solution)/shard_map/all_gather | solution.py:160
  29.2 24.5 %all-to-all-start.1 = ((f32[32,24,128]{2,1,0:T(8,128)}), f32[32,24,128]{2,1,0:T(8,128)S(1)}, u32[]{:S(2)}, u32[]{:S(2)}) async-start(f32[32,24,128]{2,1,0:T(8,128)} %broadcast_in_dim.11), calls=%async_computation.1 | async-start | bytes 786432 | tf_op jit(solution)/shard_map/all_to_all | solution.py:168
  54.9 30.8 %all-to-all-start.2 = ((f32[32,24,128]{2,1,0:T(8,128)}), f32[32,24,128]{2,1,0:T(8,128)S(1)}, u32[]{:S(2)}, u32[]{:S(2)}) async-start(f32[32,24,128]{2,1,0:T(8,128)} %get-tuple-element.56), calls=%async_computation.2 | async-start | bytes 786432 | tf_op jit(solution)/shard_map/all_to_all | solution.py:168
  110.9 17.6 %all-to-all-start.4 = ((f32[32,24,128]{2,1,0:T(8,128)}), f32[32,24,128]{2,1,0:T(8,128)S(1)}, u32[]{:S(2)}, u32[]{:S(2)}) async-start(f32[32,24,128]{2,1,0:T(8,128)} %get-tuple-element.61), calls=%async_computation.4 | async-start | bytes 786432 | tf_op jit(solution)/shard_map/all_to_all | solution.py:168
  129.7 18.7 %all-to-all-start.5 = ((f32[32,24,128]{2,1,0:T(8,128)}), f32[32,24,128]{2,1,0:T(8,128)S(1)}, u32[]{:S(2)}, u32[]{:S(2)}) async-start(f32[32,24,128]{2,1,0:T(8,128)} %get-tuple-element.66), calls=%async_computation.5 | async-start | bytes 786432 | tf_op jit(solution)/shard_map/all_to_all | solution.py:168
  135.5 167.3 %all-gather.23.cloned.1.call-start = ((), (), s32[]{:S(2)}) async-start(), calls=%async_computation.24 | async-start | bytes 4718592 | tf_op jit(solution)/shard_map/all_gather | solution.py:160
  149.6 18.2 %all-to-all-start.6 = ((f32[32,24,128]{2,1,0:T(8,128)}), f32[32,24,128]{2,1,0:T(8,128)S(1)}, u32[]{:S(2)}, u32[]{:S(2)}) async-start(f32[32,24,128]{2,1,0:T(8,128)} %get-tuple-element.68), calls=%async_computation.6 | async-start | bytes 786432 | tf_op jit(solution)/shard_map/all_to_all | solution.py:168
  187.6 18.4 %all-to-all-start.8 = ((f32[32,24,128]{2,1,0:T(8,128)}), f32[32,24,128]{2,1,0:T(8,128)S(1)}, u32[]{:S(2)}, u32[]{:S(2)}) async-start(f32[32,24,128]{2,1,0:T(8,128)} %get-tuple-element.74), calls=%async_computation.8 | async-start | bytes 786432 | tf_op jit(solution)/shard_map/all_to_all | solution.py:168
  225.0 18.2 %all-to-all-start.10 = ((f32[32,24,128]{2,1,0:T(8,128)}), f32[32,24,128]{2,1,0:T(8,128)S(1)}, u32[]{:S(2)}, u32[]{:S(2)}) async-start(f32[32,24,128]{2,1,0:T(8,128)} %get-tuple-element.80), calls=%async_computation.10 | async-start | bytes 786432 | tf_op jit(solution)/shard_map/all_to_all | solution.py:168
  262.3 17.1 %all-to-all-start.12 = ((f32[32,24,128]{2,1,0:T(8,128)}), f32[32,24,128]{2,1,0:T(8,128)S(1)}, u32[]{:S(2)}, u32[]{:S(2)}) async-start(f32[32,24,128]{2,1,0:T(8,128)} %get-tuple-element.86), calls=%async_computation.12 | async-start | bytes 786432 | tf_op jit(solution)/shard_map/all_to_all | solution.py:168
  279.9 18.1 %copy-start = (bf16[96,2048]{1,0:T(8,128)(2,1)}, bf16[96,2048]{1,0:T(8,128)(2,1)S(1)}, u32[]{:S(2)}) copy-start(bf16[96,2048]{1,0:T(8,128)(2,1)S(1)} %get-tuple-element.93.refs_14_) | copy-start | bytes 1179652
  298.0 16.2 %all-to-all-start.14 = ((f32[32,24,128]{2,1,0:T(8,128)}), f32[32,24,128]{2,1,0:T(8,128)S(1)}, u32[]{:S(2)}, u32[]{:S(2)}) async-start(f32[32,24,128]{2,1,0:T(8,128)} %get-tuple-element.92), calls=%async_computation.14 | async-start | bytes 786432 | tf_op jit(solution)/shard_map/all_to_all | solution.py:168
  302.8 1.0 copy-start.1
Sparse Core Ops, SparseCore 0:
  9.2 38.7 all-gather.8
  49.8 34.5 all-gather.10
  86.3 34.5 all-gather.12
  122.6 34.5 all-gather.14
  158.9 34.5 all-gather.16
  195.3 34.5 all-gather.18
  231.7 34.5 all-gather.20
  268.2 34.5 all-gather.22

commit v5 on v4

--- a/solution.py
+++ b/solution.py
@@ -155,28 +155,30 @@
     )(right_side[0])
     given = lax.all_to_all(chunks, "sec", 0, 0, tiled=True)
 
-    def panel(factor, d):
-        own = lax.dynamic_index_in_dim(factor, jnp.minimum(segment + d, sections - 1), 0, False)
-        return lax.all_gather(own, "sec", axis=0)
-
-    inverses = lax.all_gather(inverse_blocks[0], "sec", axis=0)
-    panels = {1: panel(factor, 1)}
+    def diagonal(factor, d):
+        return lax.dynamic_index_in_dim(factor, jnp.minimum(segment + d, sections - 1), 0, False)
+
+    first = lax.all_gather(jnp.stack([inverse_blocks[0], diagonal(factor, 1)]), "sec", axis=0)
+    panels = {1: (first, 1)}
     given, factor = lax.optimization_barrier((given, factor))
-    panels |= {d: panel(factor, d) for d in range(2, sections)}
+    for group in ((2,), (3,), (4, 5), (6, 7)):
+        sent = jnp.stack([diagonal(factor, d) for d in group])
+        gathered = lax.all_gather(sent, "sec", axis=0)
+        panels |= {d: (gathered, line) for line, d in enumerate(group)}
 
     def exchange(copies):
         return lax.all_to_all(copies, "row", 0, 0, tiled=True)
 
     def fetch(i):
         return pl.pallas_call(
-            functools.partial(fetch_kernel, i),
+            functools.partial(fetch_kernel, (i, 0)),
             out_shape=matrix_in_vmem,
             in_specs=[HBM],
             out_specs=VMEM,
             scratch_shapes=[pltpu.SemaphoreType.DMA],
             compiler_params=params,
             name=f"fetch_{i}",
-        )(in_hbm(inverses))
+        )(in_hbm(first))
 
     def apply(i, gathered, inverse):
         return pl.pallas_call(
@@ -212,10 +214,16 @@
         )(in_vmem(gathered), in_vmem(base), in_vmem(matrix))
 
     def earlier(j, base, known):
-        arrays = [inverses, *(panels[j - k] for k in range(j))]
-        places = [(1 + k, k) for k in range(j)]
-        return pl.pallas_call(
-            functools.partial(earlier_kernel, places, len(arrays), j),
+        arrays = [first]
+        places = []
+        for k in range(j):
+            array, line = panels[j - k]
+            if not any(array is other for other in arrays):
+                arrays.append(array)
+            index = [array is other for other in arrays].index(True)
+            places.append((index, (k, line)))
+        return pl.pallas_call(
+            functools.partial(earlier_kernel, places, len(arrays), (j, 0)),
             out_shape=(tile_in_vmem, matrix_in_vmem, matrix_in_vmem),
             in_specs=[VMEM] + [HBM] * len(arrays) + [VMEM] * len(known),
             out_specs=(VMEM, VMEM, VMEM),

time: 355 us -> 353 us (level)
  waiting for transfers between devices: 113 us -> 98.7 us
  blocking collectives: 123 us -> 136 us
  other arithmetic: 0 us -> 4.28 us
    all_gather x8 -> x5, waiting for transfers between devices: 40.3 us -> 27 us  [the longest x1 26.9 us: shards(): lax.all_gather(jnp.stack([inverse_blocks[0], diagonal(factor, 1)]), 'sec'...]
    all_to_all x6 -> x7, blocking collectives: 109 us -> 119 us  [exchange(): return lax.all_to_all(copies, 'row', 0, 0, tiled=True)]
    another operation x0 -> x3, other arithmetic: none -> 4.28 us  [the longest x1 2.17 us: shards(): jnp.stack([inverse_blocks[0], diagonal(factor, 1)])]
    all_to_all x9 -> x8, waiting for transfers between devices: 63.6 us -> 66 us  [exchange(): return lax.all_to_all(copies, 'row', 0, 0, tiled=True)]
    all_to_all x9 -> x8, starting transfers between devices: 54.1 us -> 53 us  [exchange(): return lax.all_to_all(copies, 'row', 0, 0, tiled=True)]
  transfers between devices with their start and end apart: 18 -> 14, of which waited for: 15 -> 9; matrix products, arithmetic and copies ran while one was open for 2% -> 2% of each run, Pallas kernels for 9% -> 9%
where the time goes in v5:
time: 353 us; the launch traced here: 352 us
  blocking collectives  136 us (39%)
  waiting for transfers between devices  98.7 us (28%)
  starting transfers between devices  59.6 us (17%)
  Pallas kernels  34.3 us (10%)
  between operations  13.4 us (4%)
  local copies, waits for them, and re-layouts  5.95 us (2%)
  other arithmetic  4.28 us (1%)
    all_to_all x7, blocking collectives, exchange(): return lax.all_to_all(copies, 'row', 0, 0, tiled=True)  119 us
    all_to_all x8, waiting for transfers between devices, exchange(): return lax.all_to_all(copies, 'row', 0, 0, tiled=True)  66 us
    all_to_all x8, starting transfers between devices, exchange(): return lax.all_to_all(copies, 'row', 0, 0, tiled=True)  53 us
    all_gather x1, waiting for transfers between devices, shards(): lax.all_gather(jnp.stack([inverse_blocks[0], diagonal(factor, 1)]), 'sec'...  26.9 us
    pallas_call x7, Pallas kernels, earlier(): pl.pallas_call(functools.partial(earlier_kernel, places, len(arrays), (j,...  18.9 us
    all_to_all x1, blocking collectives, shards(): found = lax.all_to_all(stacked, 'sec', 0, 0, tiled=True)  16.6 us
    pallas_call x7, Pallas kernels, apply(): pl.pallas_call(apply_kernel, out_shape=(tile_in_vmem, copies_in_vmem), in...  8.49 us
  transfers between devices with their start and end apart: 14, of which 9 were waited for; matrix products, arithmetic and copies ran while one was open for 2% of the time, Pallas kernels for 9%

profile of v5, /device:TPU:1, one launch (start us, length us, event | category | flops | bytes accessed | tf_op | source)
XLA Modules:
  0.0 352.0 jit_solution(10915931574494090001)
XLA Ops:
  10.6 6.5 %all-to-all-start = ((f32[8,24,128]{2,1,0:T(8,128)}), f32[8,24,128]{2,1,0:T(8,128)S(1)}, u32[]{:S(2)}, u32[]{:S(2)}) async-start(f32[8,24,128]{2,1,0:T(8,128)} %pack.1), calls=%async_computation | async-start | bytes 196608 | tf_op jit(solution)/shard_map/all_to_all | solution.py:156
  29.0 10.5 %all-to-all-start.1 = ((f32[32,24,128]{2,1,0:T(8,128)}), f32[32,24,128]{2,1,0:T(8,128)S(1)}, u32[]{:S(2)}, u32[]{:S(2)}) async-start(f32[32,24,128]{2,1,0:T(8,128)} %broadcast_in_dim.11), calls=%async_computation.1 | async-start | bytes 786432 | tf_op jit(solution)/shard_map/all_to_all | solution.py:170
  39.5 26.9 %all-gather.11.cloned.1.call-done = f32[16,64,2048]{2,1,0:T(8,128)} async-done(((f32[2,64,2048]{2,1,0:T(8,128)}), f32[16,64,2048]{2,1,0:T(8,128)}) %all-gather.11.cloned.1.call-update) | async-done | bytes 8388624 | tf_op jit(solution)/shard_map/all_gather | solution.py:161
  68.7 9.6 %all-to-all-start.2 = ((f32[32,24,128]{2,1,0:T(8,128)}), f32[32,24,128]{2,1,0:T(8,128)S(1)}, u32[]{:S(2)}, u32[]{:S(2)}) async-start(f32[32,24,128]{2,1,0:T(8,128)} %get-tuple-element.56), calls=%async_computation.2 | async-start | bytes 786432 | tf_op jit(solution)/shard_map/all_to_all | solution.py:170
  79.5 12.8 %all-to-all-done.2.gathered_ref = f32[32,24,128]{2,1,0:T(8,128)S(1)} async-done(((f32[32,24,128]{2,1,0:T(8,128)}), f32[32,24,128]{2,1,0:T(8,128)S(1)}, u32[]{:S(2)}, u32[]{:S(2)}) %all-to-all-start.2) | async-done | bytes 393248 | tf_op jit(solution)/shard_map/all_to_all | solution.py:170
  92.8 17.4 %all_to_all.85.gathered_ref = f32[32,24,128]{2,1,0:T(8,128)S(1)} all-to-all(f32[32,24,128]{2,1,0:T(8,128)S(1)} %get-tuple-element.59), channel_id=1, replica_groups=mesh['sec'=8,'row'=32] {'row'}, dimensions={0} | all-to-all | bytes 786432 | tf_op jit(solution)/shard_map/all_to_all | solution.py:170
  111.4 5.8 %all-to-all-start.4 = ((f32[32,24,128]{2,1,0:T(8,128)}), f32[32,24,128]{2,1,0:T(8,128)S(1)}, u32[]{:S(2)}, u32[]{:S(2)}) async-start(f32[32,24,128]{2,1,0:T(8,128)} %get-tuple-element.61), calls=%async_computation.4 | async-start | bytes 786432 | tf_op jit(solution)/shard_map/all_to_all | solution.py:170
  118.9 11.2 %all-to-all-done.4.gathered_ref = f32[32,24,128]{2,1,0:T(8,128)S(1)} async-done(((f32[32,24,128]{2,1,0:T(8,128)}), f32[32,24,128]{2,1,0:T(8,128)S(1)}, u32[]{:S(2)}, u32[]{:S(2)}) %all-to-all-start.4) | async-done | bytes 393248 | tf_op jit(solution)/shard_map/all_to_all | solution.py:170
  130.6 18.0 %all_to_all.86.gathered_ref = f32[32,24,128]{2,1,0:T(8,128)S(1)} all-to-all(f32[32,24,128]{2,1,0:T(8,128)S(1)} %get-tuple-element.66), channel_id=1, replica_groups=mesh['sec'=8,'row'=32] {'row'}, dimensions={0} | all-to-all | bytes 786432 | tf_op jit(solution)/shard_map/all_to_all | solution.py:170
  149.8 5.8 %all-to-all-start.6 = ((f32[32,24,128]{2,1,0:T(8,128)}), f32[32,24,128]{2,1,0:T(8,128)S(1)}, u32[]{:S(2)}, u32[]{:S(2)}) async-start(f32[32,24,128]{2,1,0:T(8,128)} %get-tuple-element.68), calls=%async_computation.6 | async-start | bytes 786432 | tf_op jit(solution)/shard_map/all_to_all | solution.py:170
  157.8 10.3 %all-to-all-done.6.gathered_ref = f32[32,24,128]{2,1,0:T(8,128)S(1)} async-done(((f32[32,24,128]{2,1,0:T(8,128)}), f32[32,24,128]{2,1,0:T(8,128)S(1)}, u32[]{:S(2)}, u32[]{:S(2)}) %all-to-all-start.6) | async-done | bytes 393248 | tf_op jit(solution)/shard_map/all_to_all | solution.py:170
  168.6 18.2 %all_to_all.87.gathered_ref = f32[32,24,128]{2,1,0:T(8,128)S(1)} all-to-all(f32[32,24,128]{2,1,0:T(8,128)S(1)} %get-tuple-element.72), channel_id=1, replica_groups=mesh['sec'=8,'row'=32] {'row'}, dimensions={0} | all-to-all | bytes 786432 | tf_op jit(solution)/shard_map/all_to_all | solution.py:170
  188.0 5.7 %all-to-all-start.8 = ((f32[32,24,128]{2,1,0:T(8,128)}), f32[32,24,128]{2,1,0:T(8,128)S(1)}, u32[]{:S(2)}, u32[]{:S(2)}) async-start(f32[32,24,128]{2,1,0:T(8,128)} %get-tuple-element.74), calls=%async_computation.8 | async-start | bytes 786432 | tf_op jit(solution)/shard_map/all_to_all | solution.py:170
  196.3 9.3 %all-to-all-done.8.gathered_ref = f32[32,24,128]{2,1,0:T(8,128)S(1)} async-done(((f32[32,24,128]{2,1,0:T(8,128)}), f32[32,24,128]{2,1,0:T(8,128)S(1)}, u32[]{:S(2)}, u32[]{:S(2)}) %all-to-all-start.8) | async-done | bytes 393248 | tf_op jit(solution)/shard_map/all_to_all | solution.py:170
  206.0 17.9 %all_to_all.88.gathered_ref = f32[32,24,128]{2,1,0:T(8,128)S(1)} all-to-all(f32[32,24,128]{2,1,0:T(8,128)S(1)} %get-tuple-element.78), channel_id=1, replica_groups=mesh['sec'=8,'row'=32] {'row'}, dimensions={0} | all-to-all | bytes 786432 | tf_op jit(solution)/shard_map/all_to_all | solution.py:170
  225.2 5.9 %all-to-all-start.10 = ((f32[32,24,128]{2,1,0:T(8,128)}), f32[32,24,128]{2,1,0:T(8,128)S(1)}, u32[]{:S(2)}, u32[]{:S(2)}) async-start(f32[32,24,128]{2,1,0:T(8,128)} %get-tuple-element.80), calls=%async_computation.10 | async-start | bytes 786432 | tf_op jit(solution)/shard_map/all_to_all | solution.py:170
  234.4 8.5 %all-to-all-done.10.gathered_ref = f32[32,24,128]{2,1,0:T(8,128)S(1)} async-done(((f32[32,24,128]{2,1,0:T(8,128)}), f32[32,24,128]{2,1,0:T(8,128)S(1)}, u32[]{:S(2)}, u32[]{:S(2)}) %all-to-all-start.10) | async-done | bytes 393248 | tf_op jit(solution)/shard_map/all_to_all | solution.py:170
  243.3 16.9 %all_to_all.89.gathered_ref = f32[32,24,128]{2,1,0:T(8,128)S(1)} all-to-all(f32[32,24,128]{2,1,0:T(8,128)S(1)} %get-tuple-element.84), channel_id=1, replica_groups=mesh['sec'=8,'row'=32] {'row'}, dimensions={0} | all-to-all | bytes 786432 | tf_op jit(solution)/shard_map/all_to_all | solution.py:170
  261.4 5.8 %all-to-all-start.12 = ((f32[32,24,128]{2,1,0:T(8,128)}), f32[32,24,128]{2,1,0:T(8,128)S(1)}, u32[]{:S(2)}, u32[]{:S(2)}) async-start(f32[32,24,128]{2,1,0:T(8,128)} %get-tuple-element.86), calls=%async_computation.12 | async-start | bytes 786432 | tf_op jit(solution)/shard_map/all_to_all | solution.py:170
  270.9 7.8 %all-to-all-done.12.gathered_ref = f32[32,24,128]{2,1,0:T(8,128)S(1)} async-done(((f32[32,24,128]{2,1,0:T(8,128)}), f32[32,24,128]{2,1,0:T(8,128)S(1)}, u32[]{:S(2)}, u32[]{:S(2)}) %all-to-all-start.12) | async-done | bytes 393248 | tf_op jit(solution)/shard_map/all_to_all | solution.py:170
  279.2 15.7 %all_to_all.90.gathered_ref = f32[32,24,128]{2,1,0:T(8,128)S(1)} all-to-all(f32[32,24,128]{2,1,0:T(8,128)S(1)} %get-tuple-element.90), channel_id=1, replica_groups=mesh['sec'=8,'row'=32] {'row'}, dimensions={0} | all-to-all | bytes 786432 | tf_op jit(solution)/shard_map/all_to_all | solution.py:170
  305.3 6.1 %all-to-all-done.14.gathered_ref = f32[32,24,128]{2,1,0:T(8,128)S(1)} async-done(((f32[32,24,128]{2,1,0:T(8,128)}), f32[32,24,128]{2,1,0:T(8,128)S(1)}, u32[]{:S(2)}, u32[]{:S(2)}) %all-to-all-start.14) | async-done | bytes 393248 | tf_op jit(solution)/shard_map/all_to_all | solution.py:170
  312.5 15.2 %all_to_all.91.gathered_ref = f32[32,24,128]{2,1,0:T(8,128)S(1)} all-to-all(f32[32,24,128]{2,1,0:T(8,128)S(1)} %get-tuple-element.96), channel_id=1, replica_groups=mesh['sec'=8,'row'=32] {'row'}, dimensions={0} | all-to-all | bytes 786432 | tf_op jit(solution)/shard_map/all_to_all | solution.py:170
  328.1 16.6 %all_to_all.92.packed_ref = f32[8,24,128]{2,1,0:T(8,128)S(1)} all-to-all(f32[8,24,128]{2,1,0:T(8,128)S(1)} %apply_last.1), channel_id=1, replica_groups=mesh['sec'=8,'row'=32] {'sec'}, dimensions={0} | all-to-all | bytes 196608 | tf_op jit(solution)/shard_map/all_to_all | solution.py:254
  (55 shorter events, 54.4 us)
Async XLA Ops:
  6.5 3.3 copy-start.2
  6.5 59.8 %all-gather.11.cloned.1.call-start = ((), (), s32[]{:S(2)}) async-start(), calls=%async_computation.17 | async-start | bytes 9437184 | tf_op jit(solution)/shard_map/all_gather | solution.py:161
  10.6 11.5 %all-to-all-start = ((f32[8,24,128]{2,1,0:T(8,128)}), f32[8,24,128]{2,1,0:T(8,128)S(1)}, u32[]{:S(2)}, u32[]{:S(2)}) async-start(f32[8,24,128]{2,1,0:T(8,128)} %pack.1), calls=%async_computation | async-start | bytes 196608 | tf_op jit(solution)/shard_map/all_to_all | solution.py:156
  17.1 100.1 %all-gather.13.cloned.1.call-start = ((), (), s32[]{:S(2)}) async-start(), calls=%async_computation.18 | async-start | bytes 4718592 | tf_op jit(solution)/shard_map/all_gather | solution.py:166
  25.2 130.4 %all-gather.15.cloned.1.call-start = ((), (), s32[]{:S(2)}) async-start(), calls=%async_computation.19 | async-start | bytes 4718592 | tf_op jit(solution)/shard_map/all_gather | solution.py:166
  25.9 167.8 %all-gather.17.cloned.1.call-start = ((), (), s32[]{:S(2)}) async-start(), calls=%async_computation.20 | async-start | bytes 9437184 | tf_op jit(solution)/shard_map/all_gather | solution.py:166
  27.0 240.2 %all-gather.19.cloned.1.call-start = ((), (), s32[]{:S(2)}) async-start(), calls=%async_computation.21 | async-start | bytes 9437184 | tf_op jit(solution)/shard_map/all_gather | solution.py:166
  29.0 38.5 %all-to-all-start.1 = ((f32[32,24,128]{2,1,0:T(8,128)}), f32[32,24,128]{2,1,0:T(8,128)S(1)}, u32[]{:S(2)}, u32[]{:S(2)}) async-start(f32[32,24,128]{2,1,0:T(8,128)} %broadcast_in_dim.11), calls=%async_computation.1 | async-start | bytes 786432 | tf_op jit(solution)/shard_map/all_to_all | solution.py:170
  68.7 23.7 %all-to-all-start.2 = ((f32[32,24,128]{2,1,0:T(8,128)}), f32[32,24,128]{2,1,0:T(8,128)S(1)}, u32[]{:S(2)}, u32[]{:S(2)}) async-start(f32[32,24,128]{2,1,0:T(8,128)} %get-tuple-element.56), calls=%async_computation.2 | async-start | bytes 786432 | tf_op jit(solution)/shard_map/all_to_all | solution.py:170
  111.4 18.6 %all-to-all-start.4 = ((f32[32,24,128]{2,1,0:T(8,128)}), f32[32,24,128]{2,1,0:T(8,128)S(1)}, u32[]{:S(2)}, u32[]{:S(2)}) async-start(f32[32,24,128]{2,1,0:T(8,128)} %get-tuple-element.61), calls=%async_computation.4 | async-start | bytes 786432 | tf_op jit(solution)/shard_map/all_to_all | solution.py:170
  149.8 18.4 %all-to-all-start.6 = ((f32[32,24,128]{2,1,0:T(8,128)}), f32[32,24,128]{2,1,0:T(8,128)S(1)}, u32[]{:S(2)}, u32[]{:S(2)}) async-start(f32[32,24,128]{2,1,0:T(8,128)} %get-tuple-element.68), calls=%async_computation.6 | async-start | bytes 786432 | tf_op jit(solution)/shard_map/all_to_all | solution.py:170
  188.0 17.6 %all-to-all-start.8 = ((f32[32,24,128]{2,1,0:T(8,128)}), f32[32,24,128]{2,1,0:T(8,128)S(1)}, u32[]{:S(2)}, u32[]{:S(2)}) async-start(f32[32,24,128]{2,1,0:T(8,128)} %get-tuple-element.74), calls=%async_computation.8 | async-start | bytes 786432 | tf_op jit(solution)/shard_map/all_to_all | solution.py:170
  225.2 17.6 %all-to-all-start.10 = ((f32[32,24,128]{2,1,0:T(8,128)}), f32[32,24,128]{2,1,0:T(8,128)S(1)}, u32[]{:S(2)}, u32[]{:S(2)}) async-start(f32[32,24,128]{2,1,0:T(8,128)} %get-tuple-element.80), calls=%async_computation.10 | async-start | bytes 786432 | tf_op jit(solution)/shard_map/all_to_all | solution.py:170
  261.4 17.3 %all-to-all-start.12 = ((f32[32,24,128]{2,1,0:T(8,128)}), f32[32,24,128]{2,1,0:T(8,128)S(1)}, u32[]{:S(2)}, u32[]{:S(2)}) async-start(f32[32,24,128]{2,1,0:T(8,128)} %get-tuple-element.86), calls=%async_computation.12 | async-start | bytes 786432 | tf_op jit(solution)/shard_map/all_to_all | solution.py:170
  279.2 16.9 %copy-start = (bf16[96,2048]{1,0:T(8,128)(2,1)}, bf16[96,2048]{1,0:T(8,128)(2,1)S(1)}, u32[]{:S(2)}) copy-start(bf16[96,2048]{1,0:T(8,128)(2,1)S(1)} %get-tuple-element.93.refs_11_) | copy-start | bytes 1179652
  296.1 15.4 %all-to-all-start.14 = ((f32[32,24,128]{2,1,0:T(8,128)}), f32[32,24,128]{2,1,0:T(8,128)S(1)}, u32[]{:S(2)}, u32[]{:S(2)}) async-start(f32[32,24,128]{2,1,0:T(8,128)} %get-tuple-element.92), calls=%async_computation.14 | async-start | bytes 786432 | tf_op jit(solution)/shard_map/all_to_all | solution.py:170
  300.0 1.0 copy-start.1
Sparse Core Ops, SparseCore 0:
  10.0 56.3 all-gather.10
  68.2 34.7 all-gather.12
  104.9 34.5 all-gather.14
  141.2 52.1 all-gather.16
  195.2 52.3 all-gather.18
